TPU v7x, 256 devices: a whole 4x4x8 slice. The times are simulated.
256 devices in a mesh: rep: 1, dp: 256 (over x, y, z, core).
Axes of the slice: x: 4, y: 4, z: 8, core: 2. Of those that a mesh axis runs over, the one named last changes fastest.
Arguments:
- g_w_gate: bfloat16 [256, 2, 768, 2048], P(('rep', 'dp'))
- g_w_up: bfloat16 [256, 2, 768, 2048], P(('rep', 'dp'))
- g_w_down: bfloat16 [256, 2, 2048, 768], P(('rep', 'dp'))
- w_gate: bfloat16 [2, 768, 2048], replicated
- w_up: bfloat16 [2, 768, 2048], replicated
- w_down: bfloat16 [2, 2048, 768], replicated
- m_w_gate: float32 [2, 768, 2048], P(None, 'dp')
- m_w_up: float32 [2, 768, 2048], P(None, 'dp')
- m_w_down: float32 [2, 2048, 768], P(None, 'dp')
- v_w_gate: float32 [2, 768, 2048], P(None, 'dp')
- v_w_up: float32 [2, 768, 2048], P(None, 'dp')
- v_w_down: float32 [2, 2048, 768], P(None, 'dp')
Outputs:
- output 1: bfloat16 [2, 768, 2048], P('rep')
- output 2: bfloat16 [2, 768, 2048], P('rep')
- output 3: bfloat16 [2, 2048, 768], P('rep')
- output 4: float32 [2, 768, 2048], P('rep', 'dp')
- output 5: float32 [2, 768, 2048], P('rep', 'dp')
- output 6: float32 [2, 2048, 768], P('rep', 'dp')
- output 7: float32 [2, 768, 2048], P('rep', 'dp')
- output 8: float32 [2, 768, 2048], P('rep', 'dp')
- output 9: float32 [2, 2048, 768], P('rep', 'dp')
All inputs are finite; a program needn't handle non-finite values.
Results may differ from a plain program's by a relative error of at most 0.022.
Values are sent between devices in bfloat16 or wider.
A program may use at most 768 MiB of HBM per device.

v0:
```python
import jax
import jax.numpy as jnp
from jax import lax
from jax.sharding import PartitionSpec as P


def adamw(w, m, v, g):
    m = 0.9 * m + 0.1 * g
    v = 0.95 * v + 0.05 * g * g
    step = m * lax.rsqrt(v + 1e-8) + 0.1 * w
    return (w - 0.02 * step).astype(jnp.bfloat16), m, v


def clipped(gradients, sum_of_squares, count):
    factor = jnp.minimum(1.0, 0.5 * lax.rsqrt(sum_of_squares / count + 1e-30))
    return [g * factor for g in gradients]


def solution(mesh):
    def step(*arrays):
        terms, weights, m, v = (arrays[i : i + 3] for i in (0, 3, 6, 9))
        gradients = [lax.psum_scatter(t[0], "dp", scatter_dimension=1, tiled=True).astype(jnp.float32) for t in terms]
        squares = lax.psum(sum(jnp.sum(g * g) for g in gradients), "dp")
        gradients = clipped(gradients, squares, lax.psum(1, "dp") * sum(g.size for g in gradients))
        me = lax.axis_index("dp")
        own = [lax.dynamic_slice_in_dim(w, me * one.shape[1], one.shape[1], 1).astype(jnp.float32) for w, one in zip(weights, m, strict=True)]
        new = [adamw(w, m, v, g) for w, m, v, g in zip(own, m, v, gradients, strict=True)]
        whole = [lax.all_gather(one[0], "dp", axis=1, tiled=True) for one in new]
        return (*whole, *(one[1] for one in new), *(one[2] for one in new))

    all_of, cut = P(None, None, None), P(None, "dp", None)
    return jax.shard_map(
        step,
        mesh=mesh,
        in_specs=(P(("rep", "dp"), None, None, None),) * 3 + (all_of,) * 3 + (cut,) * 6,
        out_specs=(P("rep", None, None),) * 3 + (P("rep", "dp", None),) * 6,
        check_vma=False,
    )
```

profile of v0, /device:TPU:1, one launch (start us, length us, event | category | flops | bytes accessed | tf_op | source)
XLA Modules:
  0.0 1170.5 jit_solution(1686279663581536763)
XLA Ops:
  7.2 0.0 all-reduce.5.cloned.1.call-start
  7.2 0.0 copy-start
  7.2 12.8 %copy.48 = bf16[1,2,768,2048]{3,1,2,0:T(2,128)(2,1)} copy(bf16[1,2,768,2048]{3,2,1,0:T(8,128)(2,1)} %param.12) | data formatting | bytes 12582912 | tf_op args[0]
  20.0 0.0 copy-done
  20.0 18.8 %copy.47 = bf16[1,2,768,2048]{3,1,2,0:T(2,128)(2,1)} copy(bf16[1,2,768,2048]{3,2,1,0:T(8,128)(2,1)S(1)} %copy-done) | data formatting | bytes 12582912 | tf_op args[1]
  38.8 0.0 all-reduce.5.cloned.1.call-update
  38.8 0.0 reduce-scatter.4.cloned.1.call-start
  38.8 12.0 %copy.33 = bf16[2,2048,768]{2,0,1:T(2,128)(2,1)S(1)} copy(bf16[2,2048,768]{2,1,0:T(8,128)(2,1)} %bitcast.15) | data formatting | bytes 12582912
  50.8 4.1 copy.37
  54.9 0.0 copy-start.1
  54.9 0.0 copy-start.2
  54.9 0.0 copy-start.3
  54.9 0.0 copy-start.4
  54.9 0.0 copy-start.5
  54.9 0.0 copy-start.6
  54.9 0.0 reduce-scatter.4.cloned.1.call-update
  54.9 0.0 all-gather.4.cloned.1.call-start
  55.0 274.5 %all-reduce.5.cloned.1.call-done = (bf16[2,768,2048]{2,0,1:T(2,128)(2,1)}, bf16[2,768,2048]{2,0,1:T(2,128)(2,1)}) async-done(((bf16[2,768,2048]{2,0,1:T(2,128)(2,1)}, bf16[2,768,2048]{2,0,1:T(2,128)(2,1)}), (bf16[2,768,2048]{2,0,1:T(2,128)(2,1)}, bf16[2,768,2048]{2,0,1:T(2,128)(2,1)})) %all-reduce.5.cloned.1.call-update) | async-done | bytes 12582928
  329.5 1.4 fusion.8
  332.2 399.2 %reduce-scatter.4.cloned.1.call-done = bf16[8,1536]{1,0:T(8,128)(2,1)} async-done(((bf16[2048,1536]{1,0:T(8,128)(2,1)}), bf16[8,1536]{1,0:T(8,128)(2,1)}) %reduce-scatter.4.cloned.1.call-update) | async-done | bytes 24592
  731.4 0.7 reshape.19
  732.1 0.6 fusion.10
  733.4 1.0 constant_dynamic-slice_fusion
  734.4 79.2 %psum.7 = f32[]{:T(128)} all-reduce(f32[]{:T(128)S(6)} %add.65), channel_id=1, replica_groups=mesh['rep'=1,'dp'=256] {'dp'}, use_global_device_ids=true, to_apply=%region_6.0 | all-reduce | flops 1 | bytes 8 | tf_op jit(solution)/shard_map/psum | solution.py:23
  814.3 0.0 copy-done.1
  814.3 0.0 copy-done.2
  814.3 1.5 fusion.19
  815.8 0.0 all-gather.4.cloned.1.call-update
  815.9 0.0 all-gather.6.cloned.1.call-start
  815.9 0.0 copy-done.3
  815.9 0.0 copy-done.4
  815.9 1.5 fusion.20
  817.4 0.0 all-gather.6.cloned.1.call-update
  817.5 0.2 all-gather.8.cloned.1.call-start
  817.7 0.0 copy-done.5
  817.7 0.0 copy-done.6
  817.7 1.4 fusion.15
  819.1 0.0 all-gather.8.cloned.1.call-update
  819.1 110.5 %all-gather.4.cloned.1.call-done = bf16[2,768,2048]{2,0,1:T(2,128)(2,1)} async-done(((bf16[2,3,2048]{2,0,1:T(2,128)(2,1)}), bf16[2,768,2048]{2,0,1:T(2,128)(2,1)}) %all-gather.4.cloned.1.call-update) | async-done | bytes 6291472 | tf_op jit(solution)/shard_map/all_gather | solution.py:28
  929.7 8.4 copy.31
  938.1 109.7 %all-gather.6.cloned.1.call-done = bf16[2,768,2048]{2,0,1:T(2,128)(2,1)} async-done(((bf16[2,3,2048]{2,0,1:T(2,128)(2,1)}), bf16[2,768,2048]{2,0,1:T(2,128)(2,1)}) %all-gather.6.cloned.1.call-update) | async-done | bytes 6291472 | tf_op jit(solution)/shard_map/all_gather | solution.py:28
  1047.8 8.4 copy.32
  1056.2 101.9 %all-gather.8.cloned.1.call-done = bf16[2,2048,768]{2,1,0:T(8,128)(2,1)} async-done(((bf16[2,8,768]{2,1,0:T(8,128)(2,1)}), bf16[2,2048,768]{2,1,0:T(8,128)(2,1)}) %all-gather.8.cloned.1.call-update) | async-done | bytes 6291472 | tf_op jit(solution)/shard_map/all_gather | solution.py:28
  1158.1 5.9 copy.52
Async XLA Ops:
  7.2 322.3 %all-reduce.5.cloned.1.call-start = ((), (), s32[]{:S(2)}) async-start(), calls=%async_computation.5 | async-start | bytes 25165824
  7.2 12.8 %copy-start = (bf16[1,2,768,2048]{3,2,1,0:T(8,128)(2,1)S(1)}, bf16[1,2,768,2048]{3,2,1,0:T(8,128)(2,1)}, u32[]{:S(2)}) copy-start(bf16[1,2,768,2048]{3,2,1,0:T(8,128)(2,1)} %param.13) | copy-start | bytes 18874372
  38.8 692.6 %reduce-scatter.4.cloned.1.call-start = ((), (), s32[]{:S(2)}) async-start(), calls=%async_computation.4 | async-start | bytes 6316032
  54.9 759.4 %copy-start.1 = (f32[2,3,2048]{2,0,1:T(2,128)S(1)}, f32[2,3,2048]{2,0,1:T(2,128)}, u32[]{:S(2)}) copy-start(f32[2,3,2048]{2,0,1:T(2,128)} %param.21) | copy-start | bytes 147460
  54.9 759.4 %copy-start.2 = (f32[2,3,2048]{2,0,1:T(2,128)S(1)}, f32[2,3,2048]{2,0,1:T(2,128)}, u32[]{:S(2)}) copy-start(f32[2,3,2048]{2,0,1:T(2,128)} %param.18) | copy-start | bytes 147460
  54.9 761.0 %copy-start.3 = (f32[2,3,2048]{2,0,1:T(2,128)S(1)}, f32[2,3,2048]{2,0,1:T(2,128)}, u32[]{:S(2)}) copy-start(f32[2,3,2048]{2,0,1:T(2,128)} %param.22) | copy-start | bytes 147460
  54.9 761.0 %copy-start.4 = (f32[2,3,2048]{2,0,1:T(2,128)S(1)}, f32[2,3,2048]{2,0,1:T(2,128)}, u32[]{:S(2)}) copy-start(f32[2,3,2048]{2,0,1:T(2,128)} %param.19) | copy-start | bytes 147460
  54.9 762.8 %copy-start.5 = (f32[2,8,768]{2,1,0:T(8,128)S(1)}, f32[2,8,768]{2,1,0:T(8,128)}, u32[]{:S(2)}) copy-start(f32[2,8,768]{2,1,0:T(8,128)} %param.23) | copy-start | bytes 147460
  54.9 762.8 %copy-start.6 = (f32[2,8,768]{2,1,0:T(8,128)S(1)}, f32[2,8,768]{2,1,0:T(8,128)}, u32[]{:S(2)}) copy-start(f32[2,8,768]{2,1,0:T(8,128)} %param.20) | copy-start | bytes 147460
  54.9 874.7 %all-gather.4.cloned.1.call-start = ((), (), s32[]{:S(2)}) async-start(), calls=%async_computation.1 | async-start | bytes 6316032 | tf_op jit(solution)/shard_map/all_gather | solution.py:28
  815.9 231.9 %all-gather.6.cloned.1.call-start = ((), (), s32[]{:S(2)}) async-start(), calls=%async_computation.2 | async-start | bytes 6316032 | tf_op jit(solution)/shard_map/all_gather | solution.py:28
  817.5 340.6 %all-gather.8.cloned.1.call-start = ((), (), s32[]{:S(2)}) async-start(), calls=%async_computation.3 | async-start | bytes 6316032 | tf_op jit(solution)/shard_map/all_gather | solution.py:28
Sparse Core Ops, SparseCore 0:
  38.9 290.5 all-reduce.4
  336.0 395.3 reduce-scatter.3
  816.0 113.6 all-gather.3
  933.9 113.8 all-gather.5
  1051.4 106.5 all-gather.7
where the time goes:
time: 1170 us
  waiting for transfers between devices  996 us (85%)
  blocking collectives  79.2 us (7%)
  local copies, waits for them, and re-layouts  72 us (6%)
  between operations  16.5 us (1%)
    unnamed x7, waiting for transfers between devices  674 us
    all_gather x3, waiting for transfers between devices, step(): whole = [lax.all_gather(one[0], 'dp', axis=1, tiled=True) for one in new]  322 us
    psum x1, blocking collectives, step(): squares = lax.psum(sum((jnp.sum(g * g) for g in gradients)), 'dp')  79.2 us
    unnamed x22, local copies, waits for them, and re-layouts  71 us
  transfers between devices with their start and end apart: 5, of which 5 were waited for; matrix products, arithmetic and copies ran while one was open for 3% of the time, Pallas kernels for 0%

commit v1 on v0

v1 whole, which is shorter than its diff:
```python
import math

import jax
import jax.numpy as jnp
from jax import lax
from jax.experimental import pallas as pl
from jax.experimental.pallas import tpu as pltpu
from jax.sharding import PartitionSpec as P

N, NZ, COLUMN = 4, 8, 16
LAYERS, ROWS, LANES = 2, 16, 128
TILES, WIDE, NARROW = 3, 1024, 384
SLAB = 8
F32, BF16 = jnp.float32, jnp.bfloat16
MESH = pl.DeviceIdType.MESH
BIG, SMALL = (0, 2), (2, 1)
SEMAPHORES = 201
VMEM_LIMIT = 36 * 2**20


def add_refs(dst, srcs, dims):
    @pl.loop(0, math.prod(dims))
    def _(i):
        at = []
        for d in reversed(dims):
            at.insert(0, i % d)
            i = i // d
        at = tuple(at)
        total = srcs[0][at].astype(F32)
        for s in srcs[1:]:
            total = total + s[at].astype(F32)
        dst[at] = total.astype(dst.dtype)


def order(n):
    half, seq = n // 2, []
    for s in range(1, half + 1):
        seq.append((True, s))
        if s < half:
            seq.append((False, s))
    return seq


def interleave(*some):
    live = [[next(r), r] for r in some]
    while live:
        first = min(live, key=lambda o: o[0])
        yield first[0]
        first[0] = next(first[1], None)
        if first[0] is None:
            live.remove(first)


def chain(*some):
    for one in some:
        yield from one


def run(generator):
    for _ in generator:
        pass


def tiles(part):
    return pl.ds(part[0], part[1])


def adamw(w, m, v, g):
    m = 0.9 * m + 0.1 * g
    v = 0.95 * v + 0.05 * g * g
    step = m * lax.rsqrt(v + 1e-8) + 0.1 * w
    return (w - 0.02 * step).astype(BF16), m, v


def kernel(
    gG, gU, gD, wG, wU, wD, mG, mU, mD, vG, vU, vD, oG, oU, oD, back, backD,
    ownG, peerG, ownU, peerU, ownD, peerD, accG, accU, accD, accZ, accY,
    r1G, r1U, r1D, r2G, s2G, r2U, s2U, r2D, s2D, rY, sY, rZ, sZ,
    gsum, gsumD, wcol, wcolD, mvcol, mvD, pk, pkr, pk2, nrm, nr1, nr2, sems,
):
    me = lax.axis_index("dp")
    c, k, xy = me % 2, me % COLUMN, me // COLUMN
    z, y, x = k // 2, xy % N, xy // N
    cb = c * NZ + z

    def dev(x, y, z, c):
        return {"dp": ((x * N + y) * NZ + z) * 2 + c}

    def in_column(kk):
        return {"dp": xy * COLUMN + kk}

    partner = dev(x, y, z, 1 - c)
    ring_ids = {
        "x": (dev((x + 1) % N, y, z, c), dev((x + N - 1) % N, y, z, c)),
        "y": (dev(x, (y + 1) % N, z, c), dev(x, (y + N - 1) % N, z, c)),
        "z": (dev(x, y, (z + 1) % NZ, c), dev(x, y, (z + NZ - 1) % NZ, c)),
    }
    used = []

    def sem():
        used.append(None)
        return sems.at[len(used) - 1]

    def remote(src, dst, ssem, rsem, device):
        return pltpu.make_async_remote_copy(src_ref=src, dst_ref=dst, send_sem=ssem, recv_sem=rsem, device_id=device, device_id_type=MESH)

    sent = []

    def group(ref):
        one = sem()
        sent.append((one, ref))
        return one

    def wait_all(one, ref):
        remote(ref, ref, one, one, partner).wait_recv()

    barrier = pltpu.get_barrier_semaphore()
    for j in range(1, COLUMN):
        pl.semaphore_signal(barrier, inc=1, device_id=in_column((k + j) % COLUMN), device_id_type=MESH)
        pl.semaphore_signal(barrier, inc=1, device_id={"dp": (xy + j) % COLUMN * COLUMN + k}, device_id_type=MESH)

    def wide(c):
        return pl.ds(pl.multiple_of(c * WIDE, WIDE), WIDE)

    def narrow(c):
        return pl.ds(pl.multiple_of(c * NARROW, NARROW), NARROW)

    def slab(c):
        return pl.ds(pl.multiple_of(c * SLAB, SLAB), SLAB)

    def block(mat, b, c):
        if mat == "G":
            return gG.at[:, b, :, :, :, wide(c)]
        if mat == "U":
            return gU.at[:, :, b, :, :, wide(c)]
        return gD.at[:, :, :, b, :, narrow(c)]

    own = {"G": ownG, "U": ownU, "D": ownD}
    peer = {"G": peerG, "U": peerU, "D": peerD}
    first = {"G": (x, N), "U": (y, N), "D": (z, NZ)}
    acc = {"G": accG, "U": accU, "D": accD}
    r1 = {"G": r1G, "U": r1U, "D": r1D}
    r2 = {"G": r2G, "U": r2U, "D": r2D}
    s2 = {"G": s2G, "U": s2U, "D": s2D}
    need = [("D", 4), ("G", 2), ("U", 2), ("D", 3), ("D", -3), ("D", 2), ("D", -2), ("G", 1), ("G", -1),
            ("U", 1), ("U", -1), ("D", 1), ("D", -1), ("G", 0), ("U", 0), ("D", 0)]

    def at(mat, off):
        p, n = first[mat]
        return (p + off + n) % n

    loaded = {mat: sem() for mat in own}
    for mat, off in need:
        b = at(mat, off)
        pltpu.make_async_copy(block(mat, b, c), own[mat].at[b], loaded[mat]).start()
    mine = pl.ds(pl.multiple_of(cb * LANES, LANES), LANES)
    wloads = [pltpu.make_async_copy(w.at[:, x, y, :, :, mine], wcol.at[i], sem()) for i, w in enumerate((wG, wU))]
    wloads.append(pltpu.make_async_copy(wD.at[:, x, y, z, :, narrow(c)], wcolD, sem()))
    for one in wloads:
        one.start()

    for j, ref in enumerate((mG, vG, mU, vU)):
        for l in range(LAYERS):
            for q in range(COLUMN):
                pk[q, j, TILES * l : TILES * l + TILES, :] = ref[:, l, LANES * q : LANES * q + LANES]
    for j, ref in enumerate((mD, vD)):
        mvD[j, :, slab(c), :] = ref[:, :, narrow(c)]

    with jax.named_scope("barrier"):
        pl.semaphore_wait(barrier, 2 * COLUMN - 2)

    peers, by_mat = {}, {mat: group(own[mat]) for mat in own}
    for mat, off in need:
        b = at(mat, off)
        peers[mat, off] = remote(block(mat, b, 1 - c), peer[mat].at[b], by_mat[mat], sem(), partner)
        peers[mat, off].start()

    landed = set()

    def local1(mat, off, b, half):
        if mat not in landed:
            landed.add(mat)
            pltpu.make_async_copy(own[mat], own[mat], loaded[mat]).wait()
        if (mat, off) not in landed:
            landed.add((mat, off))
            peers[mat, off].wait_recv()
        return [own[mat].at[b, half], peer[mat].at[b, half]]

    def rs_ring(name, axis, n, pos, local, send, recv, cut, ssem, dims, finish, times):
        seq, copies = order(n), {}
        for i, (far, s) in enumerate(seq):
            prev = seq.index((far, s - 1)) if s > 1 else None
            yield times[i]
            with jax.named_scope(f"{name}_{i}"):
                for d in range(2):
                    half = d if far else 1 - d
                    off = n // 2 - s + far
                    off = -off if d and off < n // 2 else off
                    b = (pos + off + n) % n
                    srcs = [cut(r) for r in local(off, b, half)]
                    if s > 1:
                        copies[d, prev].wait_recv()
                        srcs.append(cut(recv.at[d, prev]))
                    dst = cut(send(d, i, b, half))
                    add_refs(dst, srcs, dims)
                    copies[d, i] = remote(dst, cut(recv.at[d, i]), ssem, sem(), ring_ids[axis][d])
                    copies[d, i].start()
        yield times[-1]
        with jax.named_scope(f"{name}_end"):
            for half in range(2):
                copies[half, n - 2].wait_recv()
                copies[1 - half, n - 3].wait_recv()
                finish(half, [cut(recv.at[half, n - 2]), cut(recv.at[1 - half, n - 3])])

    def stage1(mat, axis, cut, ssem, dims, times):
        p, n = first[mat]

        def finish(half, got):
            add_refs(cut(acc[mat].at[half]), [cut(r) for r in local1(mat, 0, p, half)] + got, dims)

        return rs_ring(
            "rs" + mat + axis, axis, n, p, lambda off, b, half: local1(mat, off, b, half), lambda d, i, b, half: own[mat].at[b, half],
            r1[mat], cut, ssem, dims, finish, times,
        )

    def stage2(mat, axis, pos, cut, ssem, dims, finish, times):
        return rs_ring(
            "rs" + mat + axis, axis, N, pos, lambda off, b, half: [acc[mat].at[half, b]], lambda d, i, b, half: s2[mat].at[d, i],
            r2[mat], cut, ssem, dims, finish, times,
        )

    def to_z(which, mat, pos, part):
        def finish(half, got):
            here = acc[mat].at[half, pos, tiles(part)]

            @pl.loop(0, part[1])
            def _(i):
                total = here[i] + got[0][i].astype(F32) + got[1][i].astype(F32)
                for q in range(NZ):
                    one = total[:, LANES * q : LANES * q + LANES]
                    accZ[q, half, which, part[0] + i] = one
                    sZ[q, half, which, part[0] + i] = one.astype(BF16)

        return finish

    ss = {key: group(r) for key, r in (("G1", r1G), ("U1", r1U), ("D1", r1D), ("G2", r2G), ("U2", r2U), ("D2", r2D))}
    ss["Z"], ss["Y"] = group(rZ.at[: NZ - 1]), group(rY.at[: N - 1])

    def across_z(part, times):
        got, cut = sem(), tiles(part)
        yield times[0]
        for j in range(1, NZ):
            zz = (z + j) % NZ
            remote(sZ.at[zz, :, :, cut], rZ.at[z, :, :, cut], ss["Z"], got, dev(x, y, zz, c)).start()
        yield times[1]
        with jax.named_scope("rsZ"):
            wait_all(got, rZ.at[: NZ - 1, :, :, cut])

            @pl.loop(0, 2 * LAYERS)
            def _(i):
                half, which = i // 2, i % 2
                for t in range(part[0], sum(part)):
                    total = accZ[z, half, which, t]
                    for j in range(1, NZ):
                        total = total + rZ[(z + j) % NZ, half, which, t].astype(F32)
                    gsum[half, which, t] = total.astype(BF16).astype(F32)

    def rs_pipe(part, t1, t2, tz):
        cut1, cut2, n = (lambda r: r.at[:, tiles(part)]), (lambda r: r.at[tiles(part)]), part[1]
        return chain(
            interleave(
                chain(stage1("G", "x", cut1, ss["G1"], (N, n), t1), stage2("G", "y", y, cut2, ss["G2"], (n,), to_z(0, "G", y, part), t2)),
                chain(stage1("U", "y", cut1, ss["U1"], (N, n), t1), stage2("U", "x", x, cut2, ss["U2"], (n,), to_z(1, "U", x, part), t2)),
            ),
            across_z(part, tz),
        )

    def finishDx(half, got):
        @pl.loop(0, N)
        def _(i):
            total = accD[half, x, i] + got[0][i].astype(F32) + got[1][i].astype(F32)
            accY[half, i] = total
            sY[i, half] = total.astype(BF16)

    def across_y(times):
        got = sem()
        yield times[0]
        for j in range(1, N):
            yy = (y + j) % N
            remote(sY.at[yy], rY.at[y], ss["Y"], got, dev(x, yy, z, c)).start()
        yield times[1]
        with jax.named_scope("rsY"):
            wait_all(got, rY.at[: N - 1])
            for half in range(LAYERS):
                total = accY[half, y]
                for j in range(1, N):
                    total = total + rY[(y + j) % N, half].astype(F32)
                gsumD[half] = total.astype(BF16).astype(F32)

    whole = lambda r: r
    mv, mvd = sem(), sem()

    def send_moments():
        yield 31.0
        ssem, ssemD = group(pk.at[: COLUMN - 1]), group(mvD.at[:, :, :SLAB])
        for j in range(1, COLUMN):
            kk = (k + j) % COLUMN
            remote(pk.at[(kk % 2) * NZ + kk // 2], pkr.at[k], ssem, mv, in_column(kk)).start()
        for j, ref in enumerate((mD, vD)):
            remote(ref.at[:, :, narrow(1 - c)], mvD.at[j, :, slab(c)], ssemD, mvd, partner).start()

    run(interleave(
        chain(
            stage1("D", "z", whole, ss["D1"], (N, N), (-1.0, 0.7, 6.7, 10.9, 15.1, 19.3, 23.5, 32.0)),
            stage2("D", "x", x, whole, ss["D2"], (N,), finishDx, (32.0, 32.0, 36.2, 39.5)),
            across_y((39.5, 43.0)),
        ),
        rs_pipe(BIG, (0.0, 1.0, 8.5, 22.6), (22.6, 22.6, 29.0, 33.0), (33.0, 42.0)),
        rs_pipe(SMALL, (5.0, 12.0, 16.7, 28.2), (28.2, 28.2, 33.5, 36.5), (36.5, 44.0)),
        send_moments(),
    ))

    with jax.named_scope("norm"):
        total = jnp.zeros((SLAB, LANES), F32)

        def squares(total, g):
            for q in range(g.shape[1] // LANES):
                one = g[:, LANES * q : LANES * q + LANES]
                one = one * one
                total = total + one[:SLAB] + one[SLAB:]
            return total

        for half in range(LAYERS):
            for which in range(2):
                for t in range(TILES):
                    total = squares(total, gsum[half, which, t])
            total = squares(total, gsumD[half])
    for stage, got in enumerate((nr1, nr2)):
        with jax.named_scope(f"norm{stage}"):
            nrm[stage] = total
            here, rsem, ssem = (xy if stage else k), sem(), group(got.at[: COLUMN - 1])
            for j in range(1, COLUMN):
                there = (here + j) % COLUMN
                device = {"dp": there * COLUMN + k} if stage else in_column(there)
                remote(nrm.at[stage], got.at[here], ssem, rsem, device).start()
            if not stage:
                pkr[k] = pk[cb]
                wait_all(mv, pkr.at[: COLUMN - 1])
                for j in range(mvcol.shape[0]):
                    for l in range(LAYERS):
                        for q in range(COLUMN):
                            mvcol[j, l, TILES * q : TILES * q + TILES, :] = pkr[q, j, TILES * l : TILES * l + TILES, :]
                wait_all(mvd, mvD.at[:, :, :SLAB])
                for one in wloads:
                    one.wait()
            got[here] = nrm[stage]
            wait_all(rsem, got.at[: COLUMN - 1])
            total = got[0]
            for j in range(1, COLUMN):
                total = total + got[j]
    total = jnp.sum(jnp.sum(total, axis=1, keepdims=True), axis=0, keepdims=True)
    factor = jnp.minimum(1.0, 0.5 * lax.rsqrt(total / (3 * 2 * 768 * 2048) + 1e-30))

    with jax.named_scope("adamw"):
        for half in range(LAYERS):
            new, m, v = adamw(wcolD[half].astype(F32), mvD[0, half], mvD[1, half], gsumD[half] * factor)
            oD[half, x, y, z, :, narrow(c)] = new
            mvD[0, half] = m
            mvD[1, half] = v
            for a, out in enumerate((oG, oU)):
                for b in range(TILES):
                    rows, at_m, at_v = pl.ds(ROWS * b, ROWS), 2 * a, 2 * a + 1
                    new, m, v = adamw(
                        wcol[a, half, b].astype(F32), mvcol[at_m, half, rows], mvcol[at_v, half, rows], gsum[half, a, b] * factor
                    )
                    out[half, x, y, b, :, mine] = new
                    mvcol[at_m, half, rows] = m
                    mvcol[at_v, half, rows] = v

    onward = {mat: (group(peer[mat]), sem()) for mat in peer}

    def ag_ring(name, axis, n, pos, piece, ssem, on, times):
        seq, copies = order(n), {}

        def pass_on(ref):
            if on:
                remote(ref, ref, *onward[on], partner).start()

        def got(d, i):
            far, s = seq[i]
            copies[d, i].wait_recv()
            pass_on(piece((pos + (s if d else n - s)) % n, d if far else 1 - d))

        for i, (far, s) in enumerate(seq):
            yield times[i]
            with jax.named_scope(f"{name}_{i}"):
                for d in range(2):
                    if s > 1:
                        got(d, seq.index((far, s - 1)))
                    ref = piece((pos + (s - 1 if d else n - s + 1)) % n, d if far else 1 - d)
                    copies[d, i] = remote(ref, ref, ssem, sem(), ring_ids[axis][d])
                    copies[d, i].start()
        for half in range(2):
            pass_on(piece(pos, half))
        for slot in (n - 3, n - 2):
            yield times[slot + 2]
            with jax.named_scope(f"{name}_end{slot}"):
                for d in range(2):
                    got(d, slot)

    ss = {key: group(r) for key, r in (("G1", r1G), ("U1", r1U), ("D1", r1D), ("G2", r2G), ("U2", r2U), ("D2", r2D))}
    ss["Z"], ss["Y"] = group(rZ.at[: NZ - 1]), group(rY.at[: N - 1])

    def back_z(part, times):
        got = sem()
        yield times[0]
        for j in range(1, NZ):
            for out in (oG, oU):
                ref = out.at[:, x, y, tiles(part), :, mine]
                remote(ref, ref, ss["Z"], got, dev(x, y, (z + j) % NZ, c)).start()
        yield times[1]
        with jax.named_scope("agZ"):
            wait_all(got, rZ.at[: NZ - 1, :, :, tiles(part)])

    def back_y(times):
        got = sem()
        yield times[0]
        ref = oD.at[:, x, y, z, :, narrow(c)]
        for j in range(1, N):
            remote(ref, ref, ss["Y"], got, dev(x, (y + j) % N, z, c)).start()
        yield times[1]
        with jax.named_scope("agY"):
            wait_all(got, rY.at[: N - 1])

    def ag_pipe(part, tz, t2, t1):
        cols, cut = wide(c), tiles(part)
        return chain(
            back_z(part, tz),
            interleave(
                chain(
                    ag_ring("agGy", "y", N, y, lambda p, half: oG.at[half, x, p, cut, :, cols], ss["G2"], None, t2),
                    ag_ring("agGx", "x", N, x, lambda p, half: oG.at[half, p, :, cut, :, cols], ss["G1"], "G", t1),
                ),
                chain(
                    ag_ring("agUx", "x", N, x, lambda p, half: oU.at[half, p, y, cut, :, cols], ss["U2"], None, t2),
                    ag_ring("agUy", "y", N, y, lambda p, half: oU.at[half, :, p, cut, :, cols], ss["U1"], "U", t1),
                ),
            ),
        )

    rb, rd = sem(), sem()

    def return_moments():
        yield 14.0
        for q in range(COLUMN):
            for j in range(mvcol.shape[0]):
                for l in range(LAYERS):
                    pk2[q, j, TILES * l : TILES * l + TILES, :] = mvcol[j, l, TILES * q : TILES * q + TILES, :]
        ssem, ssemD = group(pk2.at[: COLUMN - 1]), group(backD.at[:, 0])
        for j in range(1, COLUMN):
            kk = (k + j) % COLUMN
            remote(pk2.at[kk], back.at[cb], ssem, rb, in_column(kk)).start()
        for j in range(2):
            remote(mvD.at[j, :, slab(1 - c)], backD.at[j, c], ssemD, rd, partner).start()
            backD[j, c] = mvD[j, :, slab(c)]
        back[cb] = pk2[k]

    run(interleave(
        chain(
            back_y((0.0, 4.0)),
            ag_ring("agDx", "x", N, x, lambda p, half: oD.at[half, p, :, z, :, narrow(c)], ss["D2"], None, (4.0, 4.0, 7.8, 9.2, 10.5)),
            ag_ring("agDz", "z", NZ, z, lambda p, half: oD.at[half, :, :, p, :, narrow(c)], ss["D1"], "D",
                    (10.5, 10.5, 17.3, 21.5, 25.7, 29.9, 34.1, 38.3, 42.5)),
        ),
        ag_pipe(SMALL, (0.1, 7.5), (7.5, 7.5, 10.9, 12.0, 12.6), (12.6, 12.6, 18.0, 21.0, 23.5)),
        ag_pipe(BIG, (0.2, 13.0), (13.0, 13.0, 17.2, 18.6, 20.0), (20.0, 20.0, 29.0, 35.0, 40.5)),
        return_moments(),
    ))

    with jax.named_scope("drain"):
        wait_all(rb, back.at[: COLUMN - 1])
        wait_all(rd, backD.at[:, 0])
        for mat in peer:
            wait_all(onward[mat][1], peer[mat])
        for one, ref in sent:
            remote(ref, ref, one, one, partner).wait_send()
    assert len(used) == SEMAPHORES, len(used)


def store(iG, iU, iD, packed, packedD, oG, oU, oD, omG, omU, omD, ovG, ovU, ovD, sem):
    pairs = ((iG, oG), (iU, oU), (iD, oD))
    for j, (i, o) in enumerate(pairs):
        for l in range(LAYERS):
            for p in range(N):
                pltpu.make_async_copy(i.at[l, p], o.at[l, p], sem.at[j]).start()
    for j, out in enumerate((omG, ovG, omU, ovU)):
        for l in range(LAYERS):
            for q in range(COLUMN):
                out[:, l, LANES * q : LANES * q + LANES] = packed[q, j, TILES * l : TILES * l + TILES, :]
    for j, out in enumerate((omD, ovD)):
        for h in range(2):
            out[:, :, NARROW * h : NARROW * h + NARROW] = packedD[j, h]
    for j, (i, o) in enumerate(pairs):
        pltpu.make_async_copy(i, o, sem.at[j]).wait()


def fused(*arrays):
    g, w, m, v = (arrays[i : i + 3] for i in (0, 3, 6, 9))
    big, low = (N, TILES, ROWS, WIDE), (N, N, ROWS, NARROW)
    view = (LAYERS, N, N, TILES, ROWS, 2 * WIDE)
    views = [view, view, (LAYERS, N, N, NZ, ROWS, 2 * NARROW)]
    g = [one.reshape(s) for one, s in zip(g, views, strict=True)]
    w = [one.reshape(s) for one, s in zip(w, views, strict=True)]
    m, v = ([jnp.swapaxes(one, 0, 1) if one.shape[1] == TILES else one for one in t] for t in (m, v))
    vm, hbm, D = pl.BlockSpec(memory_space=pltpu.VMEM), pl.BlockSpec(memory_space=pl.ANY), pltpu.SemaphoreType.DMA

    def V(dtype, *shape):
        return pltpu.VMEM(shape, dtype)

    tile, packed, packedD = (TILES, ROWS, LANES), (COLUMN, N, SLAB, LANES), (2, 2, LAYERS, SLAB, NARROW)
    scratch = [
        *[V(BF16, N, LAYERS, *big)] * 4, *[V(BF16, NZ, LAYERS, *low)] * 2,
        *[V(F32, LAYERS, *big)] * 2, V(F32, LAYERS, *low), V(F32, NZ, LAYERS, 2, *tile), V(F32, LAYERS, *low[1:]),
        *[V(BF16, 2, N - 1, *big)] * 2, V(BF16, 2, NZ - 1, *low),
        *[V(BF16, 2, N - 1, *big[1:])] * 4, *[V(BF16, 2, N - 1, *low[1:])] * 2,
        *[V(BF16, N, LAYERS, *low[2:])] * 2, *[V(BF16, NZ, LAYERS, 2, *tile)] * 2,
        V(F32, LAYERS, 2, *tile), V(F32, LAYERS, *low[2:]), V(BF16, 2, LAYERS, *tile), V(BF16, LAYERS, *low[2:]),
        V(F32, N, LAYERS, TILES * ROWS, LANES), V(F32, 2, LAYERS, *low[2:]), *[V(F32, *packed)] * 3,
        V(F32, 2, SLAB, LANES), *[V(F32, COLUMN, SLAB, LANES)] * 2, D((SEMAPHORES,)),
    ]
    passed = pl.pallas_call(
        kernel,
        out_shape=[V(BF16, *s) for s in views] + [V(F32, *packed), V(F32, *packedD)],
        in_specs=[hbm] * 6 + [vm] * 6,
        out_specs=[vm] * 5,
        scratch_shapes=scratch,
        compiler_params=pltpu.CompilerParams(collective_id=0, has_side_effects=True, vmem_limit_bytes=VMEM_LIMIT),
        name="step",
    )(*g, *w, *m, *v)
    outs = pl.pallas_call(
        store,
        out_shape=[jax.ShapeDtypeStruct(s, BF16) for s in views] + [jax.ShapeDtypeStruct(one.shape, F32) for one in (*m, *v)],
        in_specs=[vm] * 5,
        out_specs=[hbm] * 3 + [vm] * 6,
        scratch_shapes=[D((3,))],
        compiler_params=pltpu.CompilerParams(vmem_limit_bytes=2**20),
        name="store",
    )(*passed)
    outs = [jnp.swapaxes(o, 0, 1) if o.shape[0] == TILES else o for o in outs]
    return tuple(o.reshape(one.shape) for o, one in zip(outs, (*arrays[3:6], *arrays[6:]), strict=True))


def solution(mesh):
    all_of, cut = P(None, None, None), P(None, "dp", None)
    return jax.shard_map(
        fused,
        mesh=mesh,
        in_specs=(P(("rep", "dp"), None, None, None),) * 3 + (all_of,) * 3 + (cut,) * 6,
        out_specs=(P("rep", None, None),) * 3 + (P("rep", "dp", None),) * 6,
        check_vma=False,
    )
```

time: 1170 us -> 133 us (0.11)
  waiting for transfers between devices: 996 us -> 0 us
  Pallas kernels: 0 us -> 132 us
  blocking collectives: 79.2 us -> 0 us
  local copies, waits for them, and re-layouts: 72 us -> 0 us
  between operations: 16.5 us -> 0.65 us
    unnamed x7 -> x0, waiting for transfers between devices: 674 us -> none
    all_gather x3 -> x0, waiting for transfers between devices: 322 us -> none  [step(): whole = [lax.all_gather(one[0], 'dp', axis=1, tiled=True) for one in new]]
    pallas_call x0 -> x2, Pallas kernels: none -> 132 us  [the longest x1 125 us: fused(): pl.pallas_call(kernel, out_shape=[V(BF16, *s) for s in views] + [V(F32, *...]
    psum x1 -> x0, blocking collectives: 79.2 us -> none  [step(): squares = lax.psum(sum((jnp.sum(g * g) for g in gradients)), 'dp')]
    unnamed x22 -> x0, local copies, waits for them, and re-layouts: 71 us -> none
  transfers between devices with their start and end apart: 5 -> 0, of which waited for: 5 -> 0; matrix products, arithmetic and copies ran while one was open for 3% -> 0% of each run, Pallas kernels for 0% -> 0%
where the time goes in v1:
time: 133 us; the launch traced here: 132 us
  Pallas kernels  132 us (99%)
    pallas_call x1, Pallas kernels, fused(): pl.pallas_call(kernel, out_shape=[V(BF16, *s) for s in views] + [V(F32, *...  125 us
    pallas_call x1, Pallas kernels, fused(): pl.pallas_call(store, out_shape=[jax.ShapeDtypeStruct(s, BF16) for s in v...  7.18 us

profile of v1, /device:TPU:1, one launch (start us, length us, event | category | flops | bytes accessed | tf_op | source)
XLA Modules:
  0.0 132.4 jit_solution(12207942380660590543)
XLA Ops:
  0.6 124.6 %step.1 = (bf16[2,4,4,3,16,2048]{5,4,3,2,1,0:T(8,128)(2,1)S(1)}, bf16[2,4,4,3,16,2048]{5,4,3,2,1,0:T(8,128)(2,1)S(1)}, bf16[2,4,4,8,16,768]{5,4,3,2,1,0:T(8,128)...) custom-call(bf16[2,4,4,3,16,2048]{5,4,3,2,1,0:T(8,128)(2,1)} %bitcast.17, ...), custom_call_target="tpu_custom_call" | custom-call | tf_op jit(solution)/shard_map/step/pallas_call | solution.py:531
  125.3 7.2 %store.1 = (bf16[2,4,4,3,16,2048]{5,4,3,2,1,0:T(8,128)(2,1)}, bf16[2,4,4,3,16,2048]{5,4,3,2,1,0:T(8,128)(2,1)}, bf16[2,4,4,8,16,768]{5,4,3,2,1,0:T(8,128)(2,1)},...) custom-call(bf16[2,4,4,3,16,2048]{5,4,3,2,1,0:T(8,128)(2,1)S(1)} %ge, ...), custom_call_target="tpu_custom_call" | custom-call | tf_op jit(solution)/shard_map/store/pallas_call | solution.py:540

commit v2 on v1

--- a/solution.py
+++ b/solution.py
@@ -13,8 +13,7 @@
 SLAB = 8
 F32, BF16 = jnp.float32, jnp.bfloat16
 MESH = pl.DeviceIdType.MESH
-BIG, SMALL = (0, 2), (2, 1)
-SEMAPHORES = 201
+KEPT, REUSED = 11, 150
 VMEM_LIMIT = 36 * 2**20
 
 
@@ -62,7 +61,7 @@
 
 
 def tiles(part):
-    return pl.ds(part[0], part[1])
+    return pl.ds(part, 1)
 
 
 def adamw(w, m, v, g):
@@ -73,10 +72,10 @@
 
 
 def kernel(
-    gG, gU, gD, wG, wU, wD, mG, mU, mD, vG, vU, vD, oG, oU, oD, back, backD,
+    gG, gU, gD, wG, wU, wD, hmG, hmU, hmD, hvG, hvU, hvD, oG, oU, oD, back, backD,
     ownG, peerG, ownU, peerU, ownD, peerD, accG, accU, accD, accZ, accY,
     r1G, r1U, r1D, r2G, s2G, r2U, s2U, r2D, s2D, rY, sY, rZ, sZ,
-    gsum, gsumD, wcol, wcolD, mvcol, mvD, pk, pkr, pk2, nrm, nr1, nr2, sems,
+    gsum, gsumD, wcol, wcolD, mvcol, mvD, pk, pkr, pk2, nrm, nr1, nr2, mG, mU, vG, vU, mD, vD, kept, reused,
 ):
     me = lax.axis_index("dp")
     c, k, xy = me % 2, me % COLUMN, me // COLUMN
@@ -95,29 +94,38 @@
         "y": (dev(x, (y + 1) % N, z, c), dev(x, (y + N - 1) % N, z, c)),
         "z": (dev(x, y, (z + 1) % NZ, c), dev(x, y, (z + NZ - 1) % NZ, c)),
     }
-    used = []
+    counts, used = {"kept": 0, "reused": 0}, []
+
+    def keep():
+        counts["kept"] += 1
+        return kept.at[counts["kept"] - 1]
 
     def sem():
-        used.append(None)
-        return sems.at[len(used) - 1]
+        counts["reused"] += 1
+        used.append(counts["reused"])
+        return reused.at[counts["reused"] - 1]
 
     def remote(src, dst, ssem, rsem, device):
         return pltpu.make_async_remote_copy(src_ref=src, dst_ref=dst, send_sem=ssem, recv_sem=rsem, device_id=device, device_id_type=MESH)
 
     sent = []
 
-    def group(ref):
-        one = sem()
+    def group(ref, new=sem):
+        one = new()
         sent.append((one, ref))
         return one
 
+    def drain():
+        while sent:
+            one, ref = sent.pop(0)
+            remote(ref, ref, one, one, partner).wait_send()
+
     def wait_all(one, ref):
         remote(ref, ref, one, one, partner).wait_recv()
 
     barrier = pltpu.get_barrier_semaphore()
-    for j in range(1, COLUMN):
-        pl.semaphore_signal(barrier, inc=1, device_id=in_column((k + j) % COLUMN), device_id_type=MESH)
-        pl.semaphore_signal(barrier, inc=1, device_id={"dp": (xy + j) % COLUMN * COLUMN + k}, device_id_type=MESH)
+    for device in (partner, *(one for pair in ring_ids.values() for one in pair)):
+        pl.semaphore_signal(barrier, inc=1, device_id=device, device_id_type=MESH)
 
     def wide(c):
         return pl.ds(pl.multiple_of(c * WIDE, WIDE), WIDE)
@@ -128,12 +136,15 @@
     def slab(c):
         return pl.ds(pl.multiple_of(c * SLAB, SLAB), SLAB)
 
-    def block(mat, b, c):
+    def block(mat, b, c, part):
         if mat == "G":
-            return gG.at[:, b, :, :, :, wide(c)]
+            return gG.at[:, b, :, part, :, wide(c)]
         if mat == "U":
-            return gU.at[:, :, b, :, :, wide(c)]
+            return gU.at[:, :, b, part, :, wide(c)]
         return gD.at[:, :, :, b, :, narrow(c)]
+
+    def landing(ref, mat, b, part):
+        return ref.at[b] if mat == "D" else ref.at[b, :, :, part]
 
     own = {"G": ownG, "U": ownU, "D": ownD}
     peer = {"G": peerG, "U": peerU, "D": peerD}
@@ -142,48 +153,45 @@
     r1 = {"G": r1G, "U": r1U, "D": r1D}
     r2 = {"G": r2G, "U": r2U, "D": r2D}
     s2 = {"G": s2G, "U": s2U, "D": s2D}
-    need = [("D", 4), ("G", 2), ("U", 2), ("D", 3), ("D", -3), ("D", 2), ("D", -2), ("G", 1), ("G", -1),
-            ("U", 1), ("U", -1), ("D", 1), ("D", -1), ("G", 0), ("U", 0), ("D", 0)]
+    need = []
+    for d, offs, part in ((4, (2,), 0), (3, (1, -1), 0), (2, (2,), 1), (1, (1, -1), 1), (0, (2,), 2)):
+        need += [("D", off, 0) for off in sorted({d, -d}, reverse=True) if off > -4]
+        need += [(mat, off, part) for off in offs for mat in "GU"]
+    need += [(mat, 0, 0) for mat in "GU"] + [(mat, off, 2) for off in (1, -1) for mat in "GU"] + [(mat, 0, part) for part in (1, 2) for mat in "GU"]
 
     def at(mat, off):
         p, n = first[mat]
         return (p + off + n) % n
 
     loaded = {mat: sem() for mat in own}
-    for mat, off in need:
+    for mat, off, part in need:
         b = at(mat, off)
-        pltpu.make_async_copy(block(mat, b, c), own[mat].at[b], loaded[mat]).start()
+        pltpu.make_async_copy(block(mat, b, c, part), landing(own[mat], mat, b, part), loaded[mat]).start()
     mine = pl.ds(pl.multiple_of(cb * LANES, LANES), LANES)
-    wloads = [pltpu.make_async_copy(w.at[:, x, y, :, :, mine], wcol.at[i], sem()) for i, w in enumerate((wG, wU))]
-    wloads.append(pltpu.make_async_copy(wD.at[:, x, y, z, :, narrow(c)], wcolD, sem()))
-    for one in wloads:
+    wloads = [pltpu.make_async_copy(w.at[:, x, y, :, :, mine], wcol.at[i], keep()) for i, w in enumerate((wG, wU))]
+    wloads.append(pltpu.make_async_copy(wD.at[:, x, y, z, :, narrow(c)], wcolD, keep()))
+    mloads = [pltpu.make_async_copy(*pair, sem()) for pair in ((hmG, mG), (hvG, vG), (hmU, mU), (hvU, vU), (hmD, mD), (hvD, vD))]
+    for one in mloads + wloads:
         one.start()
 
-    for j, ref in enumerate((mG, vG, mU, vU)):
-        for l in range(LAYERS):
-            for q in range(COLUMN):
-                pk[q, j, TILES * l : TILES * l + TILES, :] = ref[:, l, LANES * q : LANES * q + LANES]
-    for j, ref in enumerate((mD, vD)):
-        mvD[j, :, slab(c), :] = ref[:, :, narrow(c)]
-
     with jax.named_scope("barrier"):
-        pl.semaphore_wait(barrier, 2 * COLUMN - 2)
+        pl.semaphore_wait(barrier, 7)
 
     peers, by_mat = {}, {mat: group(own[mat]) for mat in own}
-    for mat, off in need:
+    for mat, off, part in need:
         b = at(mat, off)
-        peers[mat, off] = remote(block(mat, b, 1 - c), peer[mat].at[b], by_mat[mat], sem(), partner)
-        peers[mat, off].start()
+        peers[mat, off, part] = remote(block(mat, b, 1 - c, part), landing(peer[mat], mat, b, part), by_mat[mat], sem(), partner)
+        peers[mat, off, part].start()
 
     landed = set()
 
-    def local1(mat, off, b, half):
+    def local1(mat, off, b, half, part):
         if mat not in landed:
             landed.add(mat)
             pltpu.make_async_copy(own[mat], own[mat], loaded[mat]).wait()
-        if (mat, off) not in landed:
-            landed.add((mat, off))
-            peers[mat, off].wait_recv()
+        if (mat, off, part) not in landed:
+            landed.add((mat, off, part))
+            peers[mat, off, part].wait_recv()
         return [own[mat].at[b, half], peer[mat].at[b, half]]
 
     def rs_ring(name, axis, n, pos, local, send, recv, cut, ssem, dims, finish, times):
@@ -212,14 +220,14 @@
                 copies[1 - half, n - 3].wait_recv()
                 finish(half, [cut(recv.at[half, n - 2]), cut(recv.at[1 - half, n - 3])])
 
-    def stage1(mat, axis, cut, ssem, dims, times):
+    def stage1(mat, axis, part, cut, ssem, dims, times):
         p, n = first[mat]
 
         def finish(half, got):
-            add_refs(cut(acc[mat].at[half]), [cut(r) for r in local1(mat, 0, p, half)] + got, dims)
+            add_refs(cut(acc[mat].at[half]), [cut(r) for r in local1(mat, 0, p, half, part)] + got, dims)
 
         return rs_ring(
-            "rs" + mat + axis, axis, n, p, lambda off, b, half: local1(mat, off, b, half), lambda d, i, b, half: own[mat].at[b, half],
+            "rs" + mat + axis, axis, n, p, lambda off, b, half: local1(mat, off, b, half, part), lambda d, i, b, half: own[mat].at[b, half],
             r1[mat], cut, ssem, dims, finish, times,
         )
 
@@ -233,13 +241,11 @@
         def finish(half, got):
             here = acc[mat].at[half, pos, tiles(part)]
 
-            @pl.loop(0, part[1])
-            def _(i):
-                total = here[i] + got[0][i].astype(F32) + got[1][i].astype(F32)
-                for q in range(NZ):
-                    one = total[:, LANES * q : LANES * q + LANES]
-                    accZ[q, half, which, part[0] + i] = one
-                    sZ[q, half, which, part[0] + i] = one.astype(BF16)
+            total = here[0] + got[0][0].astype(F32) + got[1][0].astype(F32)
+            for q in range(NZ):
+                one = total[:, LANES * q : LANES * q + LANES]
+                accZ[q, half, which, part] = one
+                sZ[q, half, which, part] = one.astype(BF16)
 
         return finish
 
@@ -259,18 +265,24 @@
             @pl.loop(0, 2 * LAYERS)
             def _(i):
                 half, which = i // 2, i % 2
-                for t in range(part[0], sum(part)):
-                    total = accZ[z, half, which, t]
-                    for j in range(1, NZ):
-                        total = total + rZ[(z + j) % NZ, half, which, t].astype(F32)
-                    gsum[half, which, t] = total.astype(BF16).astype(F32)
+                total = accZ[z, half, which, part]
+                for j in range(1, NZ):
+                    total = total + rZ[(z + j) % NZ, half, which, part].astype(F32)
+                gsum[half, which, part] = total.astype(BF16).astype(F32)
 
     def rs_pipe(part, t1, t2, tz):
-        cut1, cut2, n = (lambda r: r.at[:, tiles(part)]), (lambda r: r.at[tiles(part)]), part[1]
+        cut1, cut2 = (lambda r: r.at[:, tiles(part)]), (lambda r: r.at[tiles(part)])
+        long, short = (N, 1), (1,)
         return chain(
             interleave(
-                chain(stage1("G", "x", cut1, ss["G1"], (N, n), t1), stage2("G", "y", y, cut2, ss["G2"], (n,), to_z(0, "G", y, part), t2)),
-                chain(stage1("U", "y", cut1, ss["U1"], (N, n), t1), stage2("U", "x", x, cut2, ss["U2"], (n,), to_z(1, "U", x, part), t2)),
+                chain(
+                    stage1("G", "x", part, cut1, ss["G1"], long, t1),
+                    stage2("G", "y", y, cut2, ss["G2"], short, to_z(0, "G", y, part), t2),
+                ),
+                chain(
+                    stage1("U", "y", part, cut1, ss["U1"], long, t1),
+                    stage2("U", "x", x, cut2, ss["U2"], short, to_z(1, "U", x, part), t2),
+                ),
             ),
             across_z(part, tz),
         )
@@ -298,10 +310,19 @@
                 gsumD[half] = total.astype(BF16).astype(F32)
 
     whole = lambda r: r
-    mv, mvd = sem(), sem()
+    mv, mvd = keep(), keep()
 
     def send_moments():
-        yield 31.0
+        yield 16.0
+        for one in mloads:
+            one.wait()
+        for j, ref in enumerate((mG, vG, mU, vU)):
+            for l in range(LAYERS):
+                for q in range(COLUMN):
+                    pk[q, j, TILES * l : TILES * l + TILES, :] = ref[:, l, LANES * q : LANES * q + LANES]
+        for j, ref in enumerate((mD, vD)):
+            mvD[j, :, slab(c), :] = ref[:, :, narrow(c)]
+        yield 33.5
         ssem, ssemD = group(pk.at[: COLUMN - 1]), group(mvD.at[:, :, :SLAB])
         for j in range(1, COLUMN):
             kk = (k + j) % COLUMN
@@ -311,14 +332,19 @@
 
     run(interleave(
         chain(
-            stage1("D", "z", whole, ss["D1"], (N, N), (-1.0, 0.7, 6.7, 10.9, 15.1, 19.3, 23.5, 32.0)),
+            stage1("D", "z", 0, whole, ss["D1"], (N, N), (-1.0, 0.7, 6.7, 10.9, 15.1, 19.3, 23.5, 32.0)),
             stage2("D", "x", x, whole, ss["D2"], (N,), finishDx, (32.0, 32.0, 36.2, 39.5)),
-            across_y((39.5, 43.0)),
+            across_y((39.5, 44.0)),
         ),
-        rs_pipe(BIG, (0.0, 1.0, 8.5, 22.6), (22.6, 22.6, 29.0, 33.0), (33.0, 42.0)),
-        rs_pipe(SMALL, (5.0, 12.0, 16.7, 28.2), (28.2, 28.2, 33.5, 36.5), (36.5, 44.0)),
+        rs_pipe(0, (0.0, 0.8, 5.6, 13.8), (13.9, 13.9, 20.2, 27.2), (27.3, 38.0)),
+        rs_pipe(1, (3.0, 8.0, 11.2, 22.2), (22.3, 22.3, 29.0, 33.0), (33.0, 43.0)),
+        rs_pipe(2, (10.5, 14.5, 19.6, 28.5), (28.5, 28.5, 34.5, 37.5), (37.5, 46.0)),
         send_moments(),
     ))
+
+    with jax.named_scope("sent"):
+        drain()
+        counts["reused"] = 0
 
     with jax.named_scope("norm"):
         total = jnp.zeros((SLAB, LANES), F32)
@@ -338,7 +364,7 @@
     for stage, got in enumerate((nr1, nr2)):
         with jax.named_scope(f"norm{stage}"):
             nrm[stage] = total
-            here, rsem, ssem = (xy if stage else k), sem(), group(got.at[: COLUMN - 1])
+            here, rsem, ssem = (xy if stage else k), keep(), group(got.at[: COLUMN - 1], keep)
             for j in range(1, COLUMN):
                 there = (here + j) % COLUMN
                 device = {"dp": there * COLUMN + k} if stage else in_column(there)
@@ -408,8 +434,9 @@
                 for d in range(2):
                     got(d, slot)
 
-    ss = {key: group(r) for key, r in (("G1", r1G), ("U1", r1U), ("D1", r1D), ("G2", r2G), ("U2", r2U), ("D2", r2D))}
-    ss["Z"], ss["Y"] = group(rZ.at[: NZ - 1]), group(rY.at[: N - 1])
+    others = oD.at[:, :3, 0, :5, :, :NARROW]
+    ss = {key: group(r) for key, r in (("G1", r1G), ("U1", r1U), ("D1", r1D), ("G2", r2G), ("U2", r2U), ("D2", others))}
+    ss["Z"] = group(rZ.at[: NZ - 1])
 
     def back_z(part, times):
         got = sem()
@@ -422,15 +449,15 @@
         with jax.named_scope("agZ"):
             wait_all(got, rZ.at[: NZ - 1, :, :, tiles(part)])
 
-    def back_y(times):
+    def back_columns(times):
         got = sem()
         yield times[0]
         ref = oD.at[:, x, y, z, :, narrow(c)]
-        for j in range(1, N):
-            remote(ref, ref, ss["Y"], got, dev(x, (y + j) % N, z, c)).start()
+        for j in range(1, COLUMN):
+            remote(ref, ref, ss["D2"], got, {"dp": (xy + j) % COLUMN * COLUMN + k}).start()
         yield times[1]
-        with jax.named_scope("agY"):
-            wait_all(got, rY.at[: N - 1])
+        with jax.named_scope("agXY"):
+            wait_all(got, others)
 
     def ag_pipe(part, tz, t2, t1):
         cols, cut = wide(c), tiles(part)
@@ -448,7 +475,7 @@
             ),
         )
 
-    rb, rd = sem(), sem()
+    rb, rd = keep(), keep()
 
     def return_moments():
         yield 14.0
@@ -467,13 +494,13 @@
 
     run(interleave(
         chain(
-            back_y((0.0, 4.0)),
-            ag_ring("agDx", "x", N, x, lambda p, half: oD.at[half, p, :, z, :, narrow(c)], ss["D2"], None, (4.0, 4.0, 7.8, 9.2, 10.5)),
+            back_columns((0.0, 9.0)),
             ag_ring("agDz", "z", NZ, z, lambda p, half: oD.at[half, :, :, p, :, narrow(c)], ss["D1"], "D",
-                    (10.5, 10.5, 17.3, 21.5, 25.7, 29.9, 34.1, 38.3, 42.5)),
+                    (9.0, 9.0, 15.8, 20.0, 24.2, 28.4, 32.6, 36.8, 41.0)),
         ),
-        ag_pipe(SMALL, (0.1, 7.5), (7.5, 7.5, 10.9, 12.0, 12.6), (12.6, 12.6, 18.0, 21.0, 23.5)),
-        ag_pipe(BIG, (0.2, 13.0), (13.0, 13.0, 17.2, 18.6, 20.0), (20.0, 20.0, 29.0, 35.0, 40.5)),
+        ag_pipe(0, (0.1, 7.6), (7.6, 7.6, 11.2, 13.4, 14.4), (14.5, 14.5, 20.1, 23.0, 32.0)),
+        ag_pipe(1, (0.2, 10.4), (10.4, 10.4, 14.0, 16.5, 17.3), (17.4, 17.4, 26.5, 29.0, 40.2)),
+        ag_pipe(2, (0.3, 13.1), (13.1, 13.1, 16.8, 19.2, 23.4), (23.5, 23.5, 34.7, 37.5, 43.0)),
         return_moments(),
     ))
 
@@ -482,26 +509,28 @@
         wait_all(rd, backD.at[:, 0])
         for mat in peer:
             wait_all(onward[mat][1], peer[mat])
-        for one, ref in sent:
-            remote(ref, ref, one, one, partner).wait_send()
-    assert len(used) == SEMAPHORES, len(used)
-
-
-def store(iG, iU, iD, packed, packedD, oG, oU, oD, omG, omU, omD, ovG, ovU, ovD, sem):
-    pairs = ((iG, oG), (iU, oU), (iD, oD))
-    for j, (i, o) in enumerate(pairs):
+        drain()
+    assert (counts["kept"], max(used)) == (KEPT, REUSED), (counts["kept"], max(used))
+
+
+def store(iG, iU, iD, packed, packedD, oG, oU, oD, omG, omU, omD, ovG, ovU, ovD, tmG, tvG, tmU, tvU, tmD, tvD, sem):
+    pairs = ((iG, oG), (iU, oU), (iD, oD), (tmG, omG), (tvG, ovG), (tmU, omU), (tvU, ovU), (tmD, omD), (tvD, ovD))
+    copies = [pltpu.make_async_copy(*pair, sem.at[j]) for j, pair in enumerate(pairs)]
+    for j, (i, o) in enumerate(pairs[:3]):
         for l in range(LAYERS):
             for p in range(N):
                 pltpu.make_async_copy(i.at[l, p], o.at[l, p], sem.at[j]).start()
-    for j, out in enumerate((omG, ovG, omU, ovU)):
+    for j, out in enumerate((tmG, tvG, tmU, tvU)):
         for l in range(LAYERS):
             for q in range(COLUMN):
                 out[:, l, LANES * q : LANES * q + LANES] = packed[q, j, TILES * l : TILES * l + TILES, :]
-    for j, out in enumerate((omD, ovD)):
+    for j, out in enumerate((tmD, tvD)):
         for h in range(2):
             out[:, :, NARROW * h : NARROW * h + NARROW] = packedD[j, h]
-    for j, (i, o) in enumerate(pairs):
-        pltpu.make_async_copy(i, o, sem.at[j]).wait()
+    for one in copies[3:]:
+        one.start()
+    for one in copies:
+        one.wait()
 
 
 def fused(*arrays):
@@ -518,6 +547,7 @@
         return pltpu.VMEM(shape, dtype)
 
     tile, packed, packedD = (TILES, ROWS, LANES), (COLUMN, N, SLAB, LANES), (2, 2, LAYERS, SLAB, NARROW)
+    moments = [V(F32, *one.shape) for one in (m[0], m[1], v[0], v[1], m[2], v[2])]
     scratch = [
         *[V(BF16, N, LAYERS, *big)] * 4, *[V(BF16, NZ, LAYERS, *low)] * 2,
         *[V(F32, LAYERS, *big)] * 2, V(F32, LAYERS, *low), V(F32, NZ, LAYERS, 2, *tile), V(F32, LAYERS, *low[1:]),
@@ -526,12 +556,12 @@
         *[V(BF16, N, LAYERS, *low[2:])] * 2, *[V(BF16, NZ, LAYERS, 2, *tile)] * 2,
         V(F32, LAYERS, 2, *tile), V(F32, LAYERS, *low[2:]), V(BF16, 2, LAYERS, *tile), V(BF16, LAYERS, *low[2:]),
         V(F32, N, LAYERS, TILES * ROWS, LANES), V(F32, 2, LAYERS, *low[2:]), *[V(F32, *packed)] * 3,
-        V(F32, 2, SLAB, LANES), *[V(F32, COLUMN, SLAB, LANES)] * 2, D((SEMAPHORES,)),
+        V(F32, 2, SLAB, LANES), *[V(F32, COLUMN, SLAB, LANES)] * 2, *moments, D((KEPT,)), D((REUSED,)),
     ]
     passed = pl.pallas_call(
         kernel,
         out_shape=[V(BF16, *s) for s in views] + [V(F32, *packed), V(F32, *packedD)],
-        in_specs=[hbm] * 6 + [vm] * 6,
+        in_specs=[hbm] * 12,
         out_specs=[vm] * 5,
         scratch_shapes=scratch,
         compiler_params=pltpu.CompilerParams(collective_id=0, has_side_effects=True, vmem_limit_bytes=VMEM_LIMIT),
@@ -541,8 +571,8 @@
         store,
         out_shape=[jax.ShapeDtypeStruct(s, BF16) for s in views] + [jax.ShapeDtypeStruct(one.shape, F32) for one in (*m, *v)],
         in_specs=[vm] * 5,
-        out_specs=[hbm] * 3 + [vm] * 6,
-        scratch_shapes=[D((3,))],
+        out_specs=[hbm] * 9,
+        scratch_shapes=[*(moments[i] for i in (0, 2, 1, 3, 4, 5)), D((9,))],
         compiler_params=pltpu.CompilerParams(vmem_limit_bytes=2**20),
         name="store",
     )(*passed)

time: 133 us -> 129 us (0.970)
  Pallas kernels: 132 us -> 128 us
    pallas_call x1, Pallas kernels: 125 us -> 122 us  [fused(): pl.pallas_call(kernel, out_shape=[V(BF16, *s) for s in views] + [V(F32, *...]
where the time goes in v2:
time: 129 us
  Pallas kernels  128 us (99%)
    pallas_call x1, Pallas kernels, fused(): pl.pallas_call(kernel, out_shape=[V(BF16, *s) for s in views] + [V(F32, *...  122 us
    pallas_call x1, Pallas kernels, fused(): pl.pallas_call(store, out_shape=[jax.ShapeDtypeStruct(s, BF16) for s in v...  6.58 us

profile of v2, /device:TPU:1, one launch (start us, length us, event | category | flops | bytes accessed | tf_op | source)
XLA Modules:
  0.0 128.8 jit_solution(14754477899897996427)
XLA Ops:
  0.6 121.6 %step.1 = (bf16[2,4,4,3,16,2048]{5,4,3,2,1,0:T(8,128)(2,1)S(1)}, bf16[2,4,4,3,16,2048]{5,4,3,2,1,0:T(8,128)(2,1)S(1)}, bf16[2,4,4,8,16,768]{5,4,3,2,1,0:T(8,128)...) custom-call(bf16[2,4,4,3,16,2048]{5,4,3,2,1,0:T(8,128)(2,1)} %bitcast.17, ...), custom_call_target="tpu_custom_call" | custom-call | tf_op jit(solution)/shard_map/step/pallas_call | solution.py:561
  122.2 6.6 %store.1 = (bf16[2,4,4,3,16,2048]{5,4,3,2,1,0:T(8,128)(2,1)}, bf16[2,4,4,3,16,2048]{5,4,3,2,1,0:T(8,128)(2,1)}, bf16[2,4,4,8,16,768]{5,4,3,2,1,0:T(8,128)(2,1)},...) custom-call(bf16[2,4,4,3,16,2048]{5,4,3,2,1,0:T(8,128)(2,1)S(1)} %ge, ...), custom_call_target="tpu_custom_call" | custom-call | tf_op jit(solution)/shard_map/store/pallas_call | solution.py:570

commit v3 on v2

--- a/solution.py
+++ b/solution.py
@@ -13,7 +13,7 @@
 SLAB = 8
 F32, BF16 = jnp.float32, jnp.bfloat16
 MESH = pl.DeviceIdType.MESH
-KEPT, REUSED = 11, 150
+KEPT, REUSED = 11, 95
 VMEM_LIMIT = 36 * 2**20
 
 
@@ -60,6 +60,11 @@
         pass
 
 
+def packed_rows(j, l):
+    start = (j * LAYERS + l) * TILES
+    return slice(start, start + TILES)
+
+
 def tiles(part):
     return pl.ds(part, 1)
 
@@ -179,9 +184,10 @@
 
     peers, by_mat = {}, {mat: group(own[mat]) for mat in own}
     for mat, off, part in need:
-        b = at(mat, off)
-        peers[mat, off, part] = remote(block(mat, b, 1 - c, part), landing(peer[mat], mat, b, part), by_mat[mat], sem(), partner)
-        peers[mat, off, part].start()
+        b, key = at(mat, off), (mat, abs(off), part)
+        if key not in peers:
+            peers[key] = sem()
+        remote(block(mat, b, 1 - c, part), landing(peer[mat], mat, b, part), by_mat[mat], peers[key], partner).start()
 
     landed = set()
 
@@ -189,17 +195,29 @@
         if mat not in landed:
             landed.add(mat)
             pltpu.make_async_copy(own[mat], own[mat], loaded[mat]).wait()
-        if (mat, off, part) not in landed:
-            landed.add((mat, off, part))
-            peers[mat, off, part].wait_recv()
+        key = mat, abs(off), part
+        if key not in landed:
+            landed.add(key)
+            some = slice(0, 1 if off in (0, first[mat][1] // 2) else 2)
+            wait_all(peers[key], peer[mat].at[some] if mat == "D" else peer[mat].at[some, :, :, part])
         return [own[mat].at[b, half], peer[mat].at[b, half]]
 
-    def rs_ring(name, axis, n, pos, local, send, recv, cut, ssem, dims, finish, times):
-        seq, copies = order(n), {}
+    def rs_ring(name, axis, n, pos, local, send, recv, index, ssem, dims, finish, times):
+        seq, landing_sems = order(n), []
+
+        def cut(ref):
+            return ref.at[index] if index else ref
+
+        def wait_both(slot):
+            wait_all(landing_sems[slot], recv.at[(slice(None), slot, *index)])
+
         for i, (far, s) in enumerate(seq):
             prev = seq.index((far, s - 1)) if s > 1 else None
             yield times[i]
             with jax.named_scope(f"{name}_{i}"):
+                landing_sems.append(sem())
+                if s > 1:
+                    wait_both(prev)
                 for d in range(2):
                     half = d if far else 1 - d
                     off = n // 2 - s + far
@@ -207,34 +225,35 @@
                     b = (pos + off + n) % n
                     srcs = [cut(r) for r in local(off, b, half)]
                     if s > 1:
-                        copies[d, prev].wait_recv()
                         srcs.append(cut(recv.at[d, prev]))
                     dst = cut(send(d, i, b, half))
                     add_refs(dst, srcs, dims)
-                    copies[d, i] = remote(dst, cut(recv.at[d, i]), ssem, sem(), ring_ids[axis][d])
-                    copies[d, i].start()
+                    remote(dst, cut(recv.at[d, i]), ssem, landing_sems[i], ring_ids[axis][d]).start()
         yield times[-1]
         with jax.named_scope(f"{name}_end"):
+            wait_both(n - 3)
+            wait_both(n - 2)
             for half in range(2):
-                copies[half, n - 2].wait_recv()
-                copies[1 - half, n - 3].wait_recv()
                 finish(half, [cut(recv.at[half, n - 2]), cut(recv.at[1 - half, n - 3])])
 
-    def stage1(mat, axis, part, cut, ssem, dims, times):
+    def stage1(mat, axis, part, index, ssem, dims, times):
         p, n = first[mat]
+
+        def cut(ref):
+            return ref.at[index] if index else ref
 
         def finish(half, got):
             add_refs(cut(acc[mat].at[half]), [cut(r) for r in local1(mat, 0, p, half, part)] + got, dims)
 
         return rs_ring(
             "rs" + mat + axis, axis, n, p, lambda off, b, half: local1(mat, off, b, half, part), lambda d, i, b, half: own[mat].at[b, half],
-            r1[mat], cut, ssem, dims, finish, times,
+            r1[mat], index, ssem, dims, finish, times,
         )
 
-    def stage2(mat, axis, pos, cut, ssem, dims, finish, times):
+    def stage2(mat, axis, pos, index, ssem, dims, finish, times):
         return rs_ring(
             "rs" + mat + axis, axis, N, pos, lambda off, b, half: [acc[mat].at[half, b]], lambda d, i, b, half: s2[mat].at[d, i],
-            r2[mat], cut, ssem, dims, finish, times,
+            r2[mat], index, ssem, dims, finish, times,
         )
 
     def to_z(which, mat, pos, part):
@@ -270,18 +289,18 @@
                     total = total + rZ[(z + j) % NZ, half, which, part].astype(F32)
                 gsum[half, which, part] = total.astype(BF16).astype(F32)
 
-    def rs_pipe(part, t1, t2, tz):
-        cut1, cut2 = (lambda r: r.at[:, tiles(part)]), (lambda r: r.at[tiles(part)])
+    def rs_pipe(part, tG, tU, tz):
+        cut1, cut2 = (slice(None), tiles(part)), (tiles(part),)
         long, short = (N, 1), (1,)
         return chain(
             interleave(
                 chain(
-                    stage1("G", "x", part, cut1, ss["G1"], long, t1),
-                    stage2("G", "y", y, cut2, ss["G2"], short, to_z(0, "G", y, part), t2),
+                    stage1("G", "x", part, cut1, ss["G1"], long, tG[:N]),
+                    stage2("G", "y", y, cut2, ss["G2"], short, to_z(0, "G", y, part), tG[N:]),
                 ),
                 chain(
-                    stage1("U", "y", part, cut1, ss["U1"], long, t1),
-                    stage2("U", "x", x, cut2, ss["U2"], short, to_z(1, "U", x, part), t2),
+                    stage1("U", "y", part, cut1, ss["U1"], long, tU[:N]),
+                    stage2("U", "x", x, cut2, ss["U2"], short, to_z(1, "U", x, part), tU[N:]),
                 ),
             ),
             across_z(part, tz),
@@ -309,20 +328,19 @@
                     total = total + rY[(y + j) % N, half].astype(F32)
                 gsumD[half] = total.astype(BF16).astype(F32)
 
-    whole = lambda r: r
     mv, mvd = keep(), keep()
 
     def send_moments():
-        yield 16.0
+        yield 11.5
         for one in mloads:
             one.wait()
         for j, ref in enumerate((mG, vG, mU, vU)):
             for l in range(LAYERS):
                 for q in range(COLUMN):
-                    pk[q, j, TILES * l : TILES * l + TILES, :] = ref[:, l, LANES * q : LANES * q + LANES]
+                    pk[q, packed_rows(j, l), :] = ref[:, l, LANES * q : LANES * q + LANES]
         for j, ref in enumerate((mD, vD)):
             mvD[j, :, slab(c), :] = ref[:, :, narrow(c)]
-        yield 33.5
+        yield 61.5
         ssem, ssemD = group(pk.at[: COLUMN - 1]), group(mvD.at[:, :, :SLAB])
         for j in range(1, COLUMN):
             kk = (k + j) % COLUMN
@@ -332,13 +350,13 @@
 
     run(interleave(
         chain(
-            stage1("D", "z", 0, whole, ss["D1"], (N, N), (-1.0, 0.7, 6.7, 10.9, 15.1, 19.3, 23.5, 32.0)),
-            stage2("D", "x", x, whole, ss["D2"], (N,), finishDx, (32.0, 32.0, 36.2, 39.5)),
-            across_y((39.5, 44.0)),
+            stage1("D", "z", 0, (), ss["D1"], (N, N), (0, 5, 10, 12, 18, 22, 30, 50)),
+            stage2("D", "x", x, (), ss["D2"], (N,), finishDx, (51, 54, 59, 63)),
+            across_y((64, 66)),
         ),
-        rs_pipe(0, (0.0, 0.8, 5.6, 13.8), (13.9, 13.9, 20.2, 27.2), (27.3, 38.0)),
-        rs_pipe(1, (3.0, 8.0, 11.2, 22.2), (22.3, 22.3, 29.0, 33.0), (33.0, 43.0)),
-        rs_pipe(2, (10.5, 14.5, 19.6, 28.5), (28.5, 28.5, 34.5, 37.5), (37.5, 46.0)),
+        rs_pipe(0, (1, 3, 8, 16, 33, 38, 46, 55), (2, 4, 9, 17, 34, 37, 47, 56), (57, 65)),
+        rs_pipe(1, (6, 11, 15, 25, 28, 35, 36, 48), (7, 13, 14, 24, 26, 31, 32, 44), (49, 62)),
+        rs_pipe(2, (19, 21, 27, 39, 40, 43, 52, 58), (20, 23, 29, 41, 42, 45, 53, 60), (61, 67)),
         send_moments(),
     ))
 
@@ -361,6 +379,7 @@
                 for t in range(TILES):
                     total = squares(total, gsum[half, which, t])
             total = squares(total, gsumD[half])
+        total = jnp.sum(total, axis=0, keepdims=True)
     for stage, got in enumerate((nr1, nr2)):
         with jax.named_scope(f"norm{stage}"):
             nrm[stage] = total
@@ -375,7 +394,7 @@
                 for j in range(mvcol.shape[0]):
                     for l in range(LAYERS):
                         for q in range(COLUMN):
-                            mvcol[j, l, TILES * q : TILES * q + TILES, :] = pkr[q, j, TILES * l : TILES * l + TILES, :]
+                            mvcol[j, l, TILES * q : TILES * q + TILES, :] = pkr[q, packed_rows(j, l), :]
                 wait_all(mvd, mvD.at[:, :, :SLAB])
                 for one in wloads:
                     one.wait()
@@ -384,7 +403,7 @@
             total = got[0]
             for j in range(1, COLUMN):
                 total = total + got[j]
-    total = jnp.sum(jnp.sum(total, axis=1, keepdims=True), axis=0, keepdims=True)
+    total = jnp.sum(total, axis=1, keepdims=True)
     factor = jnp.minimum(1.0, 0.5 * lax.rsqrt(total / (3 * 2 * 768 * 2048) + 1e-30))
 
     with jax.named_scope("adamw"):
@@ -405,34 +424,34 @@
 
     onward = {mat: (group(peer[mat]), sem()) for mat in peer}
 
-    def ag_ring(name, axis, n, pos, piece, ssem, on, times):
-        seq, copies = order(n), {}
+    def ag_ring(name, axis, n, pos, piece, two, ssem, on, times):
+        seq, landing_sems = order(n), []
 
         def pass_on(ref):
             if on:
                 remote(ref, ref, *onward[on], partner).start()
 
-        def got(d, i):
+        def got(i):
             far, s = seq[i]
-            copies[d, i].wait_recv()
-            pass_on(piece((pos + (s if d else n - s)) % n, d if far else 1 - d))
+            wait_all(landing_sems[i], two)
+            for d in range(2):
+                pass_on(piece((pos + (s if d else n - s)) % n, d if far else 1 - d))
 
         for i, (far, s) in enumerate(seq):
             yield times[i]
             with jax.named_scope(f"{name}_{i}"):
+                landing_sems.append(sem())
+                if s > 1:
+                    got(seq.index((far, s - 1)))
                 for d in range(2):
-                    if s > 1:
-                        got(d, seq.index((far, s - 1)))
                     ref = piece((pos + (s - 1 if d else n - s + 1)) % n, d if far else 1 - d)
-                    copies[d, i] = remote(ref, ref, ssem, sem(), ring_ids[axis][d])
-                    copies[d, i].start()
+                    remote(ref, ref, ssem, landing_sems[i], ring_ids[axis][d]).start()
         for half in range(2):
             pass_on(piece(pos, half))
         for slot in (n - 3, n - 2):
             yield times[slot + 2]
             with jax.named_scope(f"{name}_end{slot}"):
-                for d in range(2):
-                    got(d, slot)
+                got(slot)
 
     others = oD.at[:, :3, 0, :5, :, :NARROW]
     ss = {key: group(r) for key, r in (("G1", r1G), ("U1", r1U), ("D1", r1D), ("G2", r2G), ("U2", r2U), ("D2", others))}
@@ -459,18 +478,19 @@
         with jax.named_scope("agXY"):
             wait_all(got, others)
 
-    def ag_pipe(part, tz, t2, t1):
-        cols, cut = wide(c), tiles(part)
+    def ag_pipe(part, tz, tG, tU):
+        cols, cut, n = wide(c), tiles(part), N + 1
+        two1, two2 = r1G.at[:, 0, :, cut], r2G.at[:, 0, cut]
         return chain(
             back_z(part, tz),
             interleave(
                 chain(
-                    ag_ring("agGy", "y", N, y, lambda p, half: oG.at[half, x, p, cut, :, cols], ss["G2"], None, t2),
-                    ag_ring("agGx", "x", N, x, lambda p, half: oG.at[half, p, :, cut, :, cols], ss["G1"], "G", t1),
+                    ag_ring("agGy", "y", N, y, lambda p, half: oG.at[half, x, p, cut, :, cols], two2, ss["G2"], None, tG[:n]),
+                    ag_ring("agGx", "x", N, x, lambda p, half: oG.at[half, p, :, cut, :, cols], two1, ss["G1"], "G", tG[n:]),
                 ),
                 chain(
-                    ag_ring("agUx", "x", N, x, lambda p, half: oU.at[half, p, y, cut, :, cols], ss["U2"], None, t2),
-                    ag_ring("agUy", "y", N, y, lambda p, half: oU.at[half, :, p, cut, :, cols], ss["U1"], "U", t1),
+                    ag_ring("agUx", "x", N, x, lambda p, half: oU.at[half, p, y, cut, :, cols], two2, ss["U2"], None, tU[:n]),
+                    ag_ring("agUy", "y", N, y, lambda p, half: oU.at[half, :, p, cut, :, cols], two1, ss["U1"], "U", tU[n:]),
                 ),
             ),
         )
@@ -478,11 +498,11 @@
     rb, rd = keep(), keep()
 
     def return_moments():
-        yield 14.0
+        yield 3
         for q in range(COLUMN):
             for j in range(mvcol.shape[0]):
                 for l in range(LAYERS):
-                    pk2[q, j, TILES * l : TILES * l + TILES, :] = mvcol[j, l, TILES * q : TILES * q + TILES, :]
+                    pk2[q, packed_rows(j, l), :] = mvcol[j, l, TILES * q : TILES * q + TILES, :]
         ssem, ssemD = group(pk2.at[: COLUMN - 1]), group(backD.at[:, 0])
         for j in range(1, COLUMN):
             kk = (k + j) % COLUMN
@@ -494,13 +514,12 @@
 
     run(interleave(
         chain(
-            back_columns((0.0, 9.0)),
-            ag_ring("agDz", "z", NZ, z, lambda p, half: oD.at[half, :, :, p, :, narrow(c)], ss["D1"], "D",
-                    (9.0, 9.0, 15.8, 20.0, 24.2, 28.4, 32.6, 36.8, 41.0)),
+            back_columns((4, 17)),
+            ag_ring("agDz", "z", NZ, z, lambda p, half: oD.at[half, :, :, p, :, narrow(c)], r1D.at[:, 0], ss["D1"], "D", (20, 34, 44, 51, 56, 61, 70, 73, 78)),
         ),
-        ag_pipe(0, (0.1, 7.6), (7.6, 7.6, 11.2, 13.4, 14.4), (14.5, 14.5, 20.1, 23.0, 32.0)),
-        ag_pipe(1, (0.2, 10.4), (10.4, 10.4, 14.0, 16.5, 17.3), (17.4, 17.4, 26.5, 29.0, 40.2)),
-        ag_pipe(2, (0.3, 13.1), (13.1, 13.1, 16.8, 19.2, 23.4), (23.5, 23.5, 34.7, 37.5, 43.0)),
+        ag_pipe(0, (2, 21), (23, 25, 36, 38, 48, 49, 57, 59, 68, 71), (22, 24, 35, 37, 47, 50, 58, 60, 69, 72)),
+        ag_pipe(1, (0, 5), (7, 9, 16, 19, 32, 33, 64, 65, 74, 76), (6, 8, 15, 18, 30, 31, 66, 67, 75, 77)),
+        ag_pipe(2, (1, 10), (12, 14, 27, 29, 41, 42, 45, 52, 54, 62), (11, 13, 26, 28, 40, 43, 46, 53, 55, 63)),
         return_moments(),
     ))
 
@@ -523,7 +542,7 @@
     for j, out in enumerate((tmG, tvG, tmU, tvU)):
         for l in range(LAYERS):
             for q in range(COLUMN):
-                out[:, l, LANES * q : LANES * q + LANES] = packed[q, j, TILES * l : TILES * l + TILES, :]
+                out[:, l, LANES * q : LANES * q + LANES] = packed[q, packed_rows(j, l), :]
     for j, out in enumerate((tmD, tvD)):
         for h in range(2):
             out[:, :, NARROW * h : NARROW * h + NARROW] = packedD[j, h]
@@ -546,7 +565,7 @@
     def V(dtype, *shape):
         return pltpu.VMEM(shape, dtype)
 
-    tile, packed, packedD = (TILES, ROWS, LANES), (COLUMN, N, SLAB, LANES), (2, 2, LAYERS, SLAB, NARROW)
+    tile, packed, packedD = (TILES, ROWS, LANES), (COLUMN, N * LAYERS * TILES, LANES), (2, 2, LAYERS, SLAB, NARROW)
     moments = [V(F32, *one.shape) for one in (m[0], m[1], v[0], v[1], m[2], v[2])]
     scratch = [
         *[V(BF16, N, LAYERS, *big)] * 4, *[V(BF16, NZ, LAYERS, *low)] * 2,
@@ -556,7 +575,7 @@
         *[V(BF16, N, LAYERS, *low[2:])] * 2, *[V(BF16, NZ, LAYERS, 2, *tile)] * 2,
         V(F32, LAYERS, 2, *tile), V(F32, LAYERS, *low[2:]), V(BF16, 2, LAYERS, *tile), V(BF16, LAYERS, *low[2:]),
         V(F32, N, LAYERS, TILES * ROWS, LANES), V(F32, 2, LAYERS, *low[2:]), *[V(F32, *packed)] * 3,
-        V(F32, 2, SLAB, LANES), *[V(F32, COLUMN, SLAB, LANES)] * 2, *moments, D((KEPT,)), D((REUSED,)),
+        V(F32, 2, 1, LANES), *[V(F32, COLUMN, 1, LANES)] * 2, *moments, D((KEPT,)), D((REUSED,)),
     ]
     passed = pl.pallas_call(
         kernel,

time: 129 us -> 119 us (0.922)
  Pallas kernels: 128 us -> 119 us
    pallas_call x1, Pallas kernels: 122 us -> 112 us  [fused(): pl.pallas_call(kernel, out_shape=[V(BF16, *s) for s in views] + [V(F32, *...]
where the time goes in v3:
time: 119 us
  Pallas kernels  119 us (100%)
    pallas_call x1, Pallas kernels, fused(): pl.pallas_call(kernel, out_shape=[V(BF16, *s) for s in views] + [V(F32, *...  112 us
    pallas_call x1, Pallas kernels, fused(): pl.pallas_call(store, out_shape=[jax.ShapeDtypeStruct(s, BF16) for s in v...  6.58 us

profile of v3, /device:TPU:1, one launch (start us, length us, event | category | flops | bytes accessed | tf_op | source)
XLA Modules:
  0.0 119.3 jit_solution(9325699910746863635)
XLA Ops:
  0.6 112.1 %step.1 = (bf16[2,4,4,3,16,2048]{5,4,3,2,1,0:T(8,128)(2,1)S(1)}, bf16[2,4,4,3,16,2048]{5,4,3,2,1,0:T(8,128)(2,1)S(1)}, bf16[2,4,4,8,16,768]{5,4,3,2,1,0:T(8,128)...) custom-call(bf16[2,4,4,3,16,2048]{5,4,3,2,1,0:T(8,128)(2,1)} %bitcast.17, ...), custom_call_target="tpu_custom_call" | custom-call | tf_op jit(solution)/shard_map/step/pallas_call | solution.py:580
  112.7 6.6 %store.1 = (bf16[2,4,4,3,16,2048]{5,4,3,2,1,0:T(8,128)(2,1)}, bf16[2,4,4,3,16,2048]{5,4,3,2,1,0:T(8,128)(2,1)}, bf16[2,4,4,8,16,768]{5,4,3,2,1,0:T(8,128)(2,1)},...) custom-call(bf16[2,4,4,3,16,2048]{5,4,3,2,1,0:T(8,128)(2,1)S(1)} %ge, ...), custom_call_target="tpu_custom_call" | custom-call | tf_op jit(solution)/shard_map/store/pallas_call | solution.py:589

commit v4 on v3

--- a/solution.py
+++ b/solution.py
@@ -13,7 +13,7 @@
 SLAB = 8
 F32, BF16 = jnp.float32, jnp.bfloat16
 MESH = pl.DeviceIdType.MESH
-KEPT, REUSED = 11, 95
+KEPT, REUSED = 13, 98
 VMEM_LIMIT = 36 * 2**20
 
 
@@ -70,17 +70,20 @@
 
 
 def adamw(w, m, v, g):
-    m = 0.9 * m + 0.1 * g
-    v = 0.95 * v + 0.05 * g * g
+    m, v = moments(m, v, g)
     step = m * lax.rsqrt(v + 1e-8) + 0.1 * w
     return (w - 0.02 * step).astype(BF16), m, v
 
 
+def moments(m, v, g):
+    return 0.9 * m + 0.1 * g, 0.95 * v + 0.05 * g * g
+
+
 def kernel(
-    gG, gU, gD, wG, wU, wD, hmG, hmU, hmD, hvG, hvU, hvD, oG, oU, oD, back, backD,
+    gG, gU, gD, wG, wU, wD, hmG, hmU, hmD, hvG, hvU, hvD, oG, oU, oD, omG, omU, omD, ovG, ovU, ovD,
     ownG, peerG, ownU, peerU, ownD, peerD, accG, accU, accD, accZ, accY,
     r1G, r1U, r1D, r2G, s2G, r2U, s2U, r2D, s2D, rY, sY, rZ, sZ,
-    gsum, gsumD, wcol, wcolD, mvcol, mvD, pk, pkr, pk2, nrm, nr1, nr2, mG, mU, vG, vU, mD, vD, kept, reused,
+    gsum, gsumD, wcol, wcolD, mvcol, mvD, pk, pkr, gk, gr, gkD, nrm, nr1, nr2, mG, mU, vG, vU, mD, vD, kept, reused,
 ):
     me = lax.axis_index("dp")
     c, k, xy = me % 2, me % COLUMN, me // COLUMN
@@ -271,39 +274,35 @@
     ss = {key: group(r) for key, r in (("G1", r1G), ("U1", r1U), ("D1", r1D), ("G2", r2G), ("U2", r2U), ("D2", r2D))}
     ss["Z"], ss["Y"] = group(rZ.at[: NZ - 1]), group(rY.at[: N - 1])
 
-    def across_z(part, times):
+    def across_z(which, part, times):
         got, cut = sem(), tiles(part)
         yield times[0]
         for j in range(1, NZ):
             zz = (z + j) % NZ
-            remote(sZ.at[zz, :, :, cut], rZ.at[z, :, :, cut], ss["Z"], got, dev(x, y, zz, c)).start()
+            remote(sZ.at[zz, :, which, cut], rZ.at[z, :, which, cut], ss["Z"], got, dev(x, y, zz, c)).start()
         yield times[1]
         with jax.named_scope("rsZ"):
-            wait_all(got, rZ.at[: NZ - 1, :, :, cut])
-
-            @pl.loop(0, 2 * LAYERS)
-            def _(i):
-                half, which = i // 2, i % 2
+            wait_all(got, rZ.at[: NZ - 1, :, which, cut])
+            for half in range(LAYERS):
                 total = accZ[z, half, which, part]
                 for j in range(1, NZ):
                     total = total + rZ[(z + j) % NZ, half, which, part].astype(F32)
-                gsum[half, which, part] = total.astype(BF16).astype(F32)
-
-    def rs_pipe(part, tG, tU, tz):
+                gsum[half, which, pl.ds(part * ROWS, ROWS)] = total.astype(BF16).astype(F32)
+
+    def rs_pipe(part, tG, tZG, tU, tZU):
         cut1, cut2 = (slice(None), tiles(part)), (tiles(part),)
         long, short = (N, 1), (1,)
-        return chain(
-            interleave(
-                chain(
-                    stage1("G", "x", part, cut1, ss["G1"], long, tG[:N]),
-                    stage2("G", "y", y, cut2, ss["G2"], short, to_z(0, "G", y, part), tG[N:]),
-                ),
-                chain(
-                    stage1("U", "y", part, cut1, ss["U1"], long, tU[:N]),
-                    stage2("U", "x", x, cut2, ss["U2"], short, to_z(1, "U", x, part), tU[N:]),
-                ),
+        return interleave(
+            chain(
+                stage1("G", "x", part, cut1, ss["G1"], long, tG[:N]),
+                stage2("G", "y", y, cut2, ss["G2"], short, to_z(0, "G", y, part), tG[N:]),
+                across_z(0, part, tZG),
             ),
-            across_z(part, tz),
+            chain(
+                stage1("U", "y", part, cut1, ss["U1"], long, tU[:N]),
+                stage2("U", "x", x, cut2, ss["U2"], short, to_z(1, "U", x, part), tU[N:]),
+                across_z(1, part, tZU),
+            ),
         )
 
     def finishDx(half, got):
@@ -340,7 +339,7 @@
                     pk[q, packed_rows(j, l), :] = ref[:, l, LANES * q : LANES * q + LANES]
         for j, ref in enumerate((mD, vD)):
             mvD[j, :, slab(c), :] = ref[:, :, narrow(c)]
-        yield 61.5
+        yield 66.5
         ssem, ssemD = group(pk.at[: COLUMN - 1]), group(mvD.at[:, :, :SLAB])
         for j in range(1, COLUMN):
             kk = (k + j) % COLUMN
@@ -350,13 +349,13 @@
 
     run(interleave(
         chain(
-            stage1("D", "z", 0, (), ss["D1"], (N, N), (0, 5, 10, 12, 18, 22, 30, 50)),
-            stage2("D", "x", x, (), ss["D2"], (N,), finishDx, (51, 54, 59, 63)),
-            across_y((64, 66)),
+            stage1("D", "z", 0, (), ss["D1"], (N, N), (0, 5, 10, 13, 18, 26, 30, 51)),
+            stage2("D", "x", x, (), ss["D2"], (N,), finishDx, (52, 54, 61, 68)),
+            across_y((69, 72)),
         ),
-        rs_pipe(0, (1, 3, 8, 16, 33, 38, 46, 55), (2, 4, 9, 17, 34, 37, 47, 56), (57, 65)),
-        rs_pipe(1, (6, 11, 15, 25, 28, 35, 36, 48), (7, 13, 14, 24, 26, 31, 32, 44), (49, 62)),
-        rs_pipe(2, (19, 21, 27, 39, 40, 43, 52, 58), (20, 23, 29, 41, 42, 45, 53, 60), (61, 67)),
+        rs_pipe(0, (1, 3, 8, 16, 20, 23, 28, 39), (40, 60), (2, 4, 9, 17, 19, 33, 35, 47), (48, 64)),
+        rs_pipe(1, (6, 21, 25, 41, 42, 44, 53, 62), (63, 71), (7, 27, 29, 45, 46, 50, 57, 65), (66, 73)),
+        rs_pipe(2, (11, 14, 22, 34, 36, 38, 49, 58), (59, 70), (12, 15, 24, 31, 32, 37, 43, 55), (56, 67)),
         send_moments(),
     ))
 
@@ -377,9 +376,11 @@
         for half in range(LAYERS):
             for which in range(2):
                 for t in range(TILES):
-                    total = squares(total, gsum[half, which, t])
+                    total = squares(total, gsum[half, which, ROWS * t : ROWS * t + ROWS])
             total = squares(total, gsumD[half])
         total = jnp.sum(total, axis=0, keepdims=True)
+    rb, rd = keep(), keep()
+    gk[:, 2 * LAYERS * TILES :, :] = jnp.zeros((COLUMN, N, LANES), F32)
     for stage, got in enumerate((nr1, nr2)):
         with jax.named_scope(f"norm{stage}"):
             nrm[stage] = total
@@ -398,6 +399,17 @@
                 wait_all(mvd, mvD.at[:, :, :SLAB])
                 for one in wloads:
                     one.wait()
+            else:
+                for q in range(COLUMN):
+                    for which in range(2):
+                        for l in range(LAYERS):
+                            gk[q, packed_rows(which, l), :] = gsum[l, which, TILES * q : TILES * q + TILES, :]
+                gs, gsD = group(gk.at[: COLUMN - 1], keep), group(gkD, keep)
+                for j in range(1, COLUMN):
+                    kk = (k + j) % COLUMN
+                    remote(gk.at[kk], gr.at[cb], gs, rb, in_column(kk)).start()
+                remote(gsumD.at[:, slab(1 - c)], gkD, gsD, rd, partner).start()
+                gr[cb] = gk[k]
             got[here] = nrm[stage]
             wait_all(rsem, got.at[: COLUMN - 1])
             total = got[0]
@@ -408,19 +420,15 @@
 
     with jax.named_scope("adamw"):
         for half in range(LAYERS):
-            new, m, v = adamw(wcolD[half].astype(F32), mvD[0, half], mvD[1, half], gsumD[half] * factor)
+            new, _, _ = adamw(wcolD[half].astype(F32), mvD[0, half], mvD[1, half], gsumD[half] * factor)
             oD[half, x, y, z, :, narrow(c)] = new
-            mvD[0, half] = m
-            mvD[1, half] = v
             for a, out in enumerate((oG, oU)):
                 for b in range(TILES):
-                    rows, at_m, at_v = pl.ds(ROWS * b, ROWS), 2 * a, 2 * a + 1
-                    new, m, v = adamw(
-                        wcol[a, half, b].astype(F32), mvcol[at_m, half, rows], mvcol[at_v, half, rows], gsum[half, a, b] * factor
+                    rows = pl.ds(ROWS * b, ROWS)
+                    new, _, _ = adamw(
+                        wcol[a, half, b].astype(F32), mvcol[2 * a, half, rows], mvcol[2 * a + 1, half, rows], gsum[half, a, rows] * factor
                     )
                     out[half, x, y, b, :, mine] = new
-                    mvcol[at_m, half, rows] = m
-                    mvcol[at_v, half, rows] = v
 
     onward = {mat: (group(peer[mat]), sem()) for mat in peer}
 
@@ -457,16 +465,15 @@
     ss = {key: group(r) for key, r in (("G1", r1G), ("U1", r1U), ("D1", r1D), ("G2", r2G), ("U2", r2U), ("D2", others))}
     ss["Z"] = group(rZ.at[: NZ - 1])
 
-    def back_z(part, times):
+    def back_z(out, part, times):
         got = sem()
         yield times[0]
+        ref = out.at[:, x, y, tiles(part), :, mine]
         for j in range(1, NZ):
-            for out in (oG, oU):
-                ref = out.at[:, x, y, tiles(part), :, mine]
-                remote(ref, ref, ss["Z"], got, dev(x, y, (z + j) % NZ, c)).start()
+            remote(ref, ref, ss["Z"], got, dev(x, y, (z + j) % NZ, c)).start()
         yield times[1]
         with jax.named_scope("agZ"):
-            wait_all(got, rZ.at[: NZ - 1, :, :, tiles(part)])
+            wait_all(got, rZ.at[: NZ - 1, :, 0, tiles(part)])
 
     def back_columns(times):
         got = sem()
@@ -478,78 +485,66 @@
         with jax.named_scope("agXY"):
             wait_all(got, others)
 
-    def ag_pipe(part, tz, tG, tU):
+    def ag_pipe(part, tZG, tG, tZU, tU):
         cols, cut, n = wide(c), tiles(part), N + 1
         two1, two2 = r1G.at[:, 0, :, cut], r2G.at[:, 0, cut]
-        return chain(
-            back_z(part, tz),
-            interleave(
-                chain(
-                    ag_ring("agGy", "y", N, y, lambda p, half: oG.at[half, x, p, cut, :, cols], two2, ss["G2"], None, tG[:n]),
-                    ag_ring("agGx", "x", N, x, lambda p, half: oG.at[half, p, :, cut, :, cols], two1, ss["G1"], "G", tG[n:]),
-                ),
-                chain(
-                    ag_ring("agUx", "x", N, x, lambda p, half: oU.at[half, p, y, cut, :, cols], two2, ss["U2"], None, tU[:n]),
-                    ag_ring("agUy", "y", N, y, lambda p, half: oU.at[half, :, p, cut, :, cols], two1, ss["U1"], "U", tU[n:]),
-                ),
+        return interleave(
+            chain(
+                back_z(oG, part, tZG),
+                ag_ring("agGy", "y", N, y, lambda p, half: oG.at[half, x, p, cut, :, cols], two2, ss["G2"], None, tG[:n]),
+                ag_ring("agGx", "x", N, x, lambda p, half: oG.at[half, p, :, cut, :, cols], two1, ss["G1"], "G", tG[n:]),
+            ),
+            chain(
+                back_z(oU, part, tZU),
+                ag_ring("agUx", "x", N, x, lambda p, half: oU.at[half, p, y, cut, :, cols], two2, ss["U2"], None, tU[:n]),
+                ag_ring("agUy", "y", N, y, lambda p, half: oU.at[half, :, p, cut, :, cols], two1, ss["U1"], "U", tU[n:]),
             ),
         )
 
-    rb, rd = keep(), keep()
-
-    def return_moments():
-        yield 3
-        for q in range(COLUMN):
-            for j in range(mvcol.shape[0]):
+    def new_moments():
+        yield 7
+        with jax.named_scope("moments"):
+            wait_all(rb, gr.at[: COLUMN - 1])
+            wait_all(rd, gkD)
+            for which, (m, v, om, ov) in enumerate(((mG, vG, omG, ovG), (mU, vU, omU, ovU))):
                 for l in range(LAYERS):
-                    pk2[q, packed_rows(j, l), :] = mvcol[j, l, TILES * q : TILES * q + TILES, :]
-        ssem, ssemD = group(pk2.at[: COLUMN - 1]), group(backD.at[:, 0])
-        for j in range(1, COLUMN):
-            kk = (k + j) % COLUMN
-            remote(pk2.at[kk], back.at[cb], ssem, rb, in_column(kk)).start()
-        for j in range(2):
-            remote(mvD.at[j, :, slab(1 - c)], backD.at[j, c], ssemD, rd, partner).start()
-            backD[j, c] = mvD[j, :, slab(c)]
-        back[cb] = pk2[k]
+                    for q in range(COLUMN):
+                        cols = slice(LANES * q, LANES * q + LANES)
+                        om[:, l, cols], ov[:, l, cols] = moments(m[:, l, cols], v[:, l, cols], gr[q, packed_rows(which, l), :] * factor)
+            for cols, g in ((narrow(c), gsumD[:, slab(c), :]), (narrow(1 - c), gkD[...])):
+                omD[:, :, cols], ovD[:, :, cols] = moments(mD[:, :, cols], vD[:, :, cols], g * factor)
 
     run(interleave(
         chain(
-            back_columns((4, 17)),
-            ag_ring("agDz", "z", NZ, z, lambda p, half: oD.at[half, :, :, p, :, narrow(c)], r1D.at[:, 0], ss["D1"], "D", (20, 34, 44, 51, 56, 61, 70, 73, 78)),
+            back_columns((5, 18)),
+            ag_ring("agDz", "z", NZ, z, lambda p, half: oD.at[half, :, :, p, :, narrow(c)], r1D.at[:, 0], ss["D1"], "D", (19, 20, 47, 54, 61, 67, 73, 78, 81)),
         ),
-        ag_pipe(0, (2, 21), (23, 25, 36, 38, 48, 49, 57, 59, 68, 71), (22, 24, 35, 37, 47, 50, 58, 60, 69, 72)),
-        ag_pipe(1, (0, 5), (7, 9, 16, 19, 32, 33, 64, 65, 74, 76), (6, 8, 15, 18, 30, 31, 66, 67, 75, 77)),
-        ag_pipe(2, (1, 10), (12, 14, 27, 29, 41, 42, 45, 52, 54, 62), (11, 13, 26, 28, 40, 43, 46, 53, 55, 63)),
-        return_moments(),
+        ag_pipe(0, (0, 8), (9, 10, 17, 21, 31, 32, 33, 52, 55, 68), (1, 11), (12, 13, 25, 26, 39, 40, 41, 53, 58, 72)),
+        ag_pipe(1, (4, 27), (28, 29, 43, 46, 59, 60, 65, 74, 79, 82), (6, 35), (36, 37, 56, 57, 69, 70, 71, 77, 80, 83)),
+        ag_pipe(2, (3, 22), (23, 24, 38, 42, 48, 49, 50, 62, 64, 76), (2, 14), (15, 16, 30, 34, 44, 45, 51, 63, 66, 75)),
+        new_moments(),
     ))
 
     with jax.named_scope("drain"):
-        wait_all(rb, back.at[: COLUMN - 1])
-        wait_all(rd, backD.at[:, 0])
         for mat in peer:
             wait_all(onward[mat][1], peer[mat])
         drain()
     assert (counts["kept"], max(used)) == (KEPT, REUSED), (counts["kept"], max(used))
 
 
-def store(iG, iU, iD, packed, packedD, oG, oU, oD, omG, omU, omD, ovG, ovU, ovD, tmG, tvG, tmU, tvU, tmD, tvD, sem):
-    pairs = ((iG, oG), (iU, oU), (iD, oD), (tmG, omG), (tvG, ovG), (tmU, omU), (tvU, ovU), (tmD, omD), (tvD, ovD))
-    copies = [pltpu.make_async_copy(*pair, sem.at[j]) for j, pair in enumerate(pairs)]
-    for j, (i, o) in enumerate(pairs[:3]):
-        for l in range(LAYERS):
-            for p in range(N):
-                pltpu.make_async_copy(i.at[l, p], o.at[l, p], sem.at[j]).start()
-    for j, out in enumerate((tmG, tvG, tmU, tvU)):
-        for l in range(LAYERS):
-            for q in range(COLUMN):
-                out[:, l, LANES * q : LANES * q + LANES] = packed[q, packed_rows(j, l), :]
-    for j, out in enumerate((tmD, tvD)):
-        for h in range(2):
-            out[:, :, NARROW * h : NARROW * h + NARROW] = packedD[j, h]
-    for one in copies[3:]:
-        one.start()
-    for one in copies:
-        one.wait()
+def store(*refs):
+    *refs, sem = refs
+    half = len(refs) // 2
+    pairs = list(zip(refs[:half], refs[half:], strict=True))
+    for j, (i, o) in enumerate(pairs):
+        if len(o.shape) > TILES:
+            for l in range(LAYERS):
+                for p in range(N):
+                    pltpu.make_async_copy(i.at[l, p], o.at[l, p], sem.at[j]).start()
+        else:
+            pltpu.make_async_copy(i, o, sem.at[j]).start()
+    for j, (i, o) in enumerate(pairs):
+        pltpu.make_async_copy(i, o, sem.at[j]).wait()
 
 
 def fused(*arrays):
@@ -565,23 +560,24 @@
     def V(dtype, *shape):
         return pltpu.VMEM(shape, dtype)
 
-    tile, packed, packedD = (TILES, ROWS, LANES), (COLUMN, N * LAYERS * TILES, LANES), (2, 2, LAYERS, SLAB, NARROW)
-    moments = [V(F32, *one.shape) for one in (m[0], m[1], v[0], v[1], m[2], v[2])]
+    tile, packed, rows48 = (TILES, ROWS, LANES), (COLUMN, N * LAYERS * TILES, LANES), (TILES * ROWS, LANES)
+    mine = [V(F32, *one.shape) for one in (m[0], m[1], v[0], v[1], m[2], v[2])]
     scratch = [
         *[V(BF16, N, LAYERS, *big)] * 4, *[V(BF16, NZ, LAYERS, *low)] * 2,
         *[V(F32, LAYERS, *big)] * 2, V(F32, LAYERS, *low), V(F32, NZ, LAYERS, 2, *tile), V(F32, LAYERS, *low[1:]),
         *[V(BF16, 2, N - 1, *big)] * 2, V(BF16, 2, NZ - 1, *low),
         *[V(BF16, 2, N - 1, *big[1:])] * 4, *[V(BF16, 2, N - 1, *low[1:])] * 2,
         *[V(BF16, N, LAYERS, *low[2:])] * 2, *[V(BF16, NZ, LAYERS, 2, *tile)] * 2,
-        V(F32, LAYERS, 2, *tile), V(F32, LAYERS, *low[2:]), V(BF16, 2, LAYERS, *tile), V(BF16, LAYERS, *low[2:]),
-        V(F32, N, LAYERS, TILES * ROWS, LANES), V(F32, 2, LAYERS, *low[2:]), *[V(F32, *packed)] * 3,
-        V(F32, 2, 1, LANES), *[V(F32, COLUMN, 1, LANES)] * 2, *moments, D((KEPT,)), D((REUSED,)),
+        V(F32, LAYERS, 2, *rows48), V(F32, LAYERS, *low[2:]), V(BF16, 2, LAYERS, *tile), V(BF16, LAYERS, *low[2:]),
+        V(F32, N, LAYERS, *rows48), V(F32, 2, LAYERS, *low[2:]), *[V(F32, *packed)] * 2,
+        *[V(F32, COLUMN, ROWS, LANES)] * 2, V(F32, LAYERS, SLAB, NARROW),
+        V(F32, 2, 1, LANES), *[V(F32, COLUMN, 1, LANES)] * 2, *mine, D((KEPT,)), D((REUSED,)),
     ]
     passed = pl.pallas_call(
         kernel,
-        out_shape=[V(BF16, *s) for s in views] + [V(F32, *packed), V(F32, *packedD)],
+        out_shape=[V(BF16, *s) for s in views] + [V(F32, *one.shape) for one in (*m, *v)],
         in_specs=[hbm] * 12,
-        out_specs=[vm] * 5,
+        out_specs=[vm] * 9,
         scratch_shapes=scratch,
         compiler_params=pltpu.CompilerParams(collective_id=0, has_side_effects=True, vmem_limit_bytes=VMEM_LIMIT),
         name="step",
@@ -589,9 +585,9 @@
     outs = pl.pallas_call(
         store,
         out_shape=[jax.ShapeDtypeStruct(s, BF16) for s in views] + [jax.ShapeDtypeStruct(one.shape, F32) for one in (*m, *v)],
-        in_specs=[vm] * 5,
+        in_specs=[vm] * 9,
         out_specs=[hbm] * 9,
-        scratch_shapes=[*(moments[i] for i in (0, 2, 1, 3, 4, 5)), D((9,))],
+        scratch_shapes=[D((9,))],
         compiler_params=pltpu.CompilerParams(vmem_limit_bytes=2**20),
         name="store",
     )(*passed)

time: 119 us -> 119 us (level)
  no operation moved by 1% of the time
where the time goes in v4:
time: 119 us
  Pallas kernels  118 us (99%)
    pallas_call x1, Pallas kernels, fused(): pl.pallas_call(kernel, out_shape=[V(BF16, *s) for s in views] + [V(F32, *...  112 us
    pallas_call x1, Pallas kernels, fused(): pl.pallas_call(store, out_shape=[jax.ShapeDtypeStruct(s, BF16) for s in v...  6.59 us

profile of v4, /device:TPU:1, one launch (start us, length us, event | category | flops | bytes accessed | tf_op | source)
XLA Modules:
  0.0 119.1 jit_solution(4263567634590649156)
XLA Ops:
  0.6 111.9 %step.1 = (bf16[2,4,4,3,16,2048]{5,4,3,2,1,0:T(8,128)(2,1)S(1)}, bf16[2,4,4,3,16,2048]{5,4,3,2,1,0:T(8,128)(2,1)S(1)}, bf16[2,4,4,8,16,768]{5,4,3,2,1,0:T(8,128)...) custom-call(bf16[2,4,4,3,16,2048]{5,4,3,2,1,0:T(8,128)(2,1)} %bitcas, ...), custom_call_target="tpu_custom_call" | custom-call | tf_op jit(solution)/shard_map/step/pallas_call | solution.py:576
  112.5 6.6 %store.1 = (bf16[2,4,4,3,16,2048]{5,4,3,2,1,0:T(8,128)(2,1)}, bf16[2,4,4,3,16,2048]{5,4,3,2,1,0:T(8,128)(2,1)}, bf16[2,4,4,8,16,768]{5,4,3,2,1,0:T(8,128)(2,1)},...) custom-call(bf16[2,4,4,3,16,2048]{5,4,3,2,1,0:T(8,128)(2,1)S(1)} %ge, ...), custom_call_target="tpu_custom_call" | custom-call | tf_op jit(solution)/shard_map/store/pallas_call | solution.py:585
